TPU v7x, 64 devices: a 2x2x8 block of a 4x4x8 slice. The times are simulated.
64 devices in a mesh: data: 4 (over x, y), model: 16 (over z, core).
Axes of the slice: x: 2, y: 2, z: 8, core: 2. Of those that a mesh axis runs over, the one named last changes fastest.
The devices are a block of a 4x4x8 slice.
Arguments:
- x_in: bfloat16 [16384, 2048], P(('data', 'model')), parts along dimension 0
- dy_in: bfloat16 [16384, 2048], P(('data', 'model')), parts along dimension 0
- w_query: bfloat16 [2048, 16, 128], P(None, 'model')
- w_key: bfloat16 [2048, 128], replicated
- w_value: bfloat16 [2048, 128], replicated
- w_out: bfloat16 [16, 128, 2048], P('model')
Outputs:
- output 1: bfloat16 [16384, 2048], P(('data', 'model')), parts along dimension 0
- output 2: float32 [8192, 16, 128], P('data', 'model'), parts along dimension 0
- output 3: float32 [8192, 128], P(('data', 'model')), parts along dimension 0
- output 4: float32 [8192, 128], P(('data', 'model')), parts along dimension 0
- output 5: float32 [64, 128, 2048], P(('data', 'model')), parts along dimension 0
There are 4 independent parts. A program takes and returns all parts, laid end to end along the dimension named above; an argument that names none is the same for every part.
All inputs are finite; a program needn't handle non-finite values.
Results may differ from a plain program's by a relative error of at most 0.00907.
Values are sent between devices in bfloat16 or wider.
A program may use at most 768 MiB of HBM per device.

v0:
```python
import math
import jax
import jax.numpy as jnp
from jax import lax
from jax.sharding import PartitionSpec as P


def solution(mesh):
    tok_spec = P(("data", "model"), None)

    def local_step(x_loc, dy_loc, wq_loc, w_key, w_value, wo_loc):
        head_dim = w_key.shape[1]
        score_scale = 1.0 / math.sqrt(head_dim)
        x_full = lax.all_gather(x_loc, "model", axis=0, tiled=True)
        dy_full = lax.all_gather(dy_loc, "model", axis=0, tiled=True)
        key_loc = jnp.dot(x_loc, w_key, preferred_element_type=jnp.float32).astype(jnp.bfloat16)
        value_loc = jnp.dot(x_loc, w_value, preferred_element_type=jnp.float32).astype(jnp.bfloat16)
        keys_all = lax.all_gather(key_loc, "model", axis=0, tiled=True)
        values_all = lax.all_gather(value_loc, "model", axis=0, tiled=True)
        positions = jnp.arange(x_full.shape[0])
        causal = positions[:, None] >= positions[None, :]
        queries = jnp.einsum("td,dhe->the", x_full, wq_loc, preferred_element_type=jnp.float32).astype(jnp.bfloat16)
        scores = jnp.einsum("qhe,ke->hqk", queries, keys_all, preferred_element_type=jnp.float32) * score_scale
        scores = jnp.where(causal[None], scores, -jnp.inf)
        probs_f32 = jax.nn.softmax(scores, axis=-1)
        probs_bf = probs_f32.astype(jnp.bfloat16)
        attn_out = jnp.einsum("hqk,ke->qhe", probs_bf, values_all, preferred_element_type=jnp.float32).astype(jnp.bfloat16)
        dw_out = jnp.einsum("qhe,qd->hed", attn_out, dy_full, preferred_element_type=jnp.float32)
        d_attn = jnp.einsum("qd,hed->qhe", dy_full, wo_loc, preferred_element_type=jnp.float32).astype(jnp.bfloat16)
        d_probs = jnp.einsum("qhe,ke->hqk", d_attn, values_all, preferred_element_type=jnp.float32)
        row_dot = jnp.einsum("qhe,qhe->hq", d_attn, attn_out, preferred_element_type=jnp.float32)
        d_scores = (probs_f32 * (d_probs - row_dot[:, :, None]) * score_scale).astype(jnp.bfloat16)
        d_query = jnp.einsum("hqk,ke->qhe", d_scores, keys_all, preferred_element_type=jnp.float32).astype(jnp.bfloat16)
        dk_part = jnp.einsum("hqk,qhe->ke", d_scores, queries, preferred_element_type=jnp.float32)
        dv_part = jnp.einsum("hqk,qhe->ke", probs_bf, d_attn, preferred_element_type=jnp.float32)
        d_keys = lax.psum_scatter(dk_part, "model", scatter_dimension=0, tiled=True).astype(jnp.bfloat16)
        d_values = lax.psum_scatter(dv_part, "model", scatter_dimension=0, tiled=True).astype(jnp.bfloat16)
        dw_query = jnp.einsum("td,the->dhe", x_full, d_query, preferred_element_type=jnp.float32)
        dx_part = jnp.einsum("the,dhe->td", d_query, wq_loc, preferred_element_type=jnp.float32)
        dx_sum = lax.psum_scatter(dx_part, "model", scatter_dimension=0, tiled=True)
        dx_sum = dx_sum + jnp.einsum("te,de->td", d_keys, w_key, preferred_element_type=jnp.float32)
        dx_sum = dx_sum + jnp.einsum("te,de->td", d_values, w_value, preferred_element_type=jnp.float32)
        dwk_part = jnp.einsum("td,te->de", x_loc, d_keys, preferred_element_type=jnp.float32)
        dwv_part = jnp.einsum("td,te->de", x_loc, d_values, preferred_element_type=jnp.float32)
        dw_key = lax.psum_scatter(dwk_part, "model", scatter_dimension=0, tiled=True)
        dw_value = lax.psum_scatter(dwv_part, "model", scatter_dimension=0, tiled=True)
        return (dx_sum.astype(jnp.bfloat16), dw_query, dw_key, dw_value, dw_out)

    return jax.shard_map(local_step, mesh=mesh, in_specs=(tok_spec, tok_spec, P(None, "model", None), P(None, None), P(None, None), P("model", None, None)), out_specs=(tok_spec, P("data", "model", None), tok_spec, tok_spec, P(("data", "model"), None, None)), check_vma=False)
```

profile of v0, /device:TPU:21, one launch (start us, length us, event | category | flops | bytes accessed | tf_op | source)
XLA Modules:
  0.0 722.3 jit_solution(4006541726855182828)
XLA Ops:
  7.2 0.1 all-gather.7.cloned.1.call-start
  7.3 0.7 all-gather.7.cloned.1.call-update
  8.0 0.1 all-gather.5.cloned.1.call-start
  8.1 2.4 convolution_convert_fusion.3
  10.5 0.1 all-gather.5.cloned.1.call-update
  10.5 0.1 all-gather.11.cloned.1.call-start
  10.6 0.7 all-gather.11.cloned.1.call-update
  11.3 0.1 all-gather.9.cloned.1.call-start
  11.4 2.4 convolution_convert_fusion.2
  13.8 0.1 all-gather.9.cloned.1.call-update
  13.9 0.1 reduce-scatter.10.cloned.1.call-start
  14.0 92.8 %all-gather.7.cloned.1.call-done = bf16[4096,2048]{1,0:T(8,128)(2,1)} async-done(((bf16[256,2048]{1,0:T(8,128)(2,1)}), bf16[4096,2048]{1,0:T(8,128)(2,1)}) %all-gather.7.cloned.1.call-update) | async-done | bytes 16777232 | tf_op jit(solution)/shard_map/all_gather | solution.py:14
  106.7 8.2 %convolution_convert_fusion.1 = bf16[4096,128]{1,0:T(8,128)(2,1)S(1)} fusion(bf16[4096,2048]{1,0:T(8,128)(2,1)} %all-gather.7.cloned.1.call-done, bf16[2048,1,128]{2,0,1:T(8,128)(2,1)S(1)} %copy-done), kind=kOutput, calls=%fused_computation.22 | convolution fusion | flops 2148007936 | bytes 18350080 | tf_op jit(solution)/shard_map/td,dhe->the/dot_general | solution.py:22
  115.0 27.8 %all-gather.5.cloned.1.call-done = bf16[4096,128]{1,0:T(8,128)(2,1)} async-done(((bf16[256,128]{1,0:T(8,128)(2,1)}), bf16[4096,128]{1,0:T(8,128)(2,1)}) %all-gather.5.cloned.1.call-update) | async-done | bytes 1048592 | tf_op jit(solution)/shard_map/all_gather | solution.py:18
  142.7 24.7 %fusion.4 = (f32[4096]{0:T(1024)S(1)}, f32[4096,4096]{1,0:T(8,128)}) fusion(bf16[4096,128]{1,0:T(8,128)(2,1)} %all-gather.5.cloned.1.call-done, bf16[4096,128]{1,0:T(8,128)(2,1)S(1)} %convolution_convert_fusion.1), kind=kOutput, calls=%fused_computation.9 | convolution fusion | flops 4362072064 | bytes 69222400 | tf_op jit(solution)/shard_map/qhe,ke->hqk/dot_general | solution.py:23
  167.4 21.7 %fusion.3 = f32[4096]{0:T(1024)S(1)} fusion(f32[4096,4096]{1,0:T(8,128)} %get-tuple-element.11, f32[4096]{0:T(1024)S(1)} %get-tuple-element.10), kind=kLoop, calls=%fused_computation.8 | loop fusion | flops 83881984 | bytes 67141632 | tf_op jit(solution)/shard_map/reduce_sum | solution.py:25
  189.2 45.7 %all-gather.11.cloned.1.call-done = bf16[4096,2048]{1,0:T(8,128)(2,1)} async-done(((bf16[256,2048]{1,0:T(8,128)(2,1)}), bf16[4096,2048]{1,0:T(8,128)(2,1)}) %all-gather.11.cloned.1.call-update) | async-done | bytes 16777232 | tf_op jit(solution)/shard_map/all_gather | solution.py:15
  234.9 8.2 %convolution_convert_fusion = bf16[4096,128]{1,0:T(8,128)(2,1)S(1)} fusion(bf16[4096,2048]{1,0:T(8,128)(2,1)} %all-gather.11.cloned.1.call-done, bf16[1,128,2048]{2,1,0:T(8,128)(2,1)S(1)} %copy-done.7), kind=kOutput, calls=%fused_computation.21 | convolution fusion | flops 2148007936 | bytes 18350080 | tf_op jit(solution)/shard_map/qd,hed->qhe/dot_general | solution.py:29
  243.2 30.0 %fusion.9 = f32[4096,128]{1,0:T(8,128)} fusion(bf16[4096,128]{1,0:T(8,128)(2,1)S(1)} %convolution_convert_fusion, f32[4096]{0:T(1024)S(1)} %fusion.3, f32[4096]{0:T(1024)S(1)} %get-tuple-element.10, f32[4096,4096]{1,0:T(8,128)} %get-tuple-element.11), kind=kOutput, calls=%fused_computation.14 | convolution fusion | flops 4395630592 | bytes 70287360 | tf_op jit(solution)/shard_map/hqk,qhe->ke/dot_general | solution.py:35
  273.2 1.5 copy.17
  274.6 0.1 reduce-scatter.10.cloned.1.call-update
  274.7 0.1 reduce-scatter.8.cloned.1.call-start
  274.8 0.0 all-gather.9.cloned.1.call-done
  274.8 28.5 %multiply_reduce_fusion = (f32[4096]{0:T(1024)S(1)}, bf16[4096,128]{0,1:T(8,128)(2,1)}) fusion(f32[4096,128]{0,1:T(8,128)S(1)} %copy.17, bf16[4096,128]{1,0:T(8,128)(2,1)} %all-gather.9.cloned.1.call-done, f32[4096]{0:T(1024)S(1)} %fusion.3, f32[4096]{0:T(1024)S(1)} %get-tuple-element.10, f32[4096,4096]{1,0:T(8,128)} %get-tuple-element.11), kind=kOutput, calls=%fused_computation.32 | convolution fusion | flops 4397723648 | bytes 71352320 | tf_op jit(solution)/shard_map/hqk,ke->qhe/dot_general | solution.py:27
  303.3 42.7 %fusion.1 = bf16[1,4096,4096]{1,2,0:T(8,128)(2,1)} fusion(bf16[4096,128]{1,0:T(8,128)(2,1)} %all-gather.9.cloned.1.call-done, bf16[4096,128]{1,0:T(8,128)(2,1)} %copy-done.4, f32[4096]{0:T(1024)S(1)} %get-tuple-element.12, f32[4096]{0:T(1024)S(1)} %fusion.3, f32[4096]{0:T(1024)S(1)} %get-tuple-element.10, f32[4096,4096]{1,0:T(8,128)} %get-tuple-element.11), kind=kOutput, calls=%fused_computation.3 | convolution fusion | flops 4445962240 | bytes 102809600 | tf_op jit(solution)/shard_map/qhe,ke->hqk/dot_general | solution.py:30
  346.0 16.5 %fusion.5 = f32[4096,128]{1,0:T(8,128)} fusion(bf16[4096,128]{1,0:T(8,128)(2,1)} %copy-done.8, bf16[1,4096,4096]{1,2,0:T(8,128)(2,1)} %fusion.1), kind=kOutput, calls=%fused_computation.10 | convolution fusion | flops 4294967296 | bytes 36700160 | tf_op jit(solution)/shard_map/hqk,qhe->ke/dot_general | solution.py:34
  362.5 0.1 reduce-scatter.8.cloned.1.call-update
  362.6 0.1 reduce-scatter.14.cloned.1.call-start
  362.7 2.2 convolution_bitcast_fusion.1
  364.9 0.1 reduce-scatter.14.cloned.1.call-update
  365.0 0.1 reduce-scatter.12.cloned.1.call-start
  365.1 49.6 %reduce-scatter.8.cloned.1.call-done = f32[256,128]{1,0:T(8,128)} async-done(((f32[4096,128]{1,0:T(8,128)}), f32[256,128]{1,0:T(8,128)}) %reduce-scatter.8.cloned.1.call-update) | async-done | bytes 131088 | tf_op jit(solution)/shard_map/reduce_scatter | solution.py:36
  414.6 2.2 convolution_bitcast_fusion.2
  416.9 0.1 reduce-scatter.12.cloned.1.call-update
  417.0 0.1 reduce-scatter.6.cloned.1.call-start
  417.0 13.1 %fusion.20 = bf16[4096,128]{0,1:T(8,128)(2,1)S(1)} fusion(bf16[4096,128]{1,0:T(8,128)(2,1)S(1)} %copy-done.3, bf16[1,4096,4096]{1,2,0:T(8,128)(2,1)} %fusion.1), kind=kOutput, calls=%fused_computation.23 | convolution fusion | flops 4295491584 | bytes 35651584 | tf_op jit(solution)/shard_map/hqk,ke->qhe/dot_general | solution.py:33
  430.2 13.2 %fusion.30 = f32[4096,2048]{1,0:T(8,128)} fusion(bf16[4096,128]{0,1:T(8,128)(2,1)S(1)} %fusion.20, bf16[2048,1,128]{2,0,1:T(8,128)(2,1)S(1)} %copy-done), kind=kOutput, calls=%fused_computation.36 | convolution fusion | flops 2147483648 | bytes 35127296 | tf_op jit(solution)/shard_map/the,dhe->td/dot_general | solution.py:39
  443.4 0.1 reduce-scatter.6.cloned.1.call-update
  443.5 8.1 %convolution_bitcast_fusion.3 = f32[2048,1,128]{0,2,1:T(8,128)S(1)} fusion(bf16[4096,128]{0,1:T(8,128)(2,1)S(1)} %fusion.20, bf16[4096,2048]{1,0:T(8,128)(2,1)} %all-gather.7.cloned.1.call-done), kind=kOutput, calls=%fused_computation.31 | convolution fusion | flops 2147483648 | bytes 18874368 | tf_op jit(solution)/shard_map/td,the->dhe/dot_general | solution.py:38
  451.6 1.9 copy.11
  453.5 9.4 %convolution_bitcast_fusion = f32[1,128,2048]{2,1,0:T(8,128)} fusion(bf16[4096,128]{0,1:T(8,128)(2,1)} %get-tuple-element.13, bf16[4096,2048]{1,0:T(8,128)(2,1)} %all-gather.11.cloned.1.call-done), kind=kOutput, calls=%fused_computation.28 | convolution fusion | flops 2147483648 | bytes 18874368 | tf_op jit(solution)/shard_map/qhe,qd->hed/dot_general | solution.py:28
  462.9 7.7 %reduce-scatter.14.cloned.1.call-done = f32[128,128]{0,1:T(8,128)} async-done(((f32[2048,128]{0,1:T(8,128)}), f32[128,128]{0,1:T(8,128)}) %reduce-scatter.14.cloned.1.call-update) | async-done | bytes 65552 | tf_op jit(solution)/shard_map/reduce_scatter | solution.py:46
  470.6 1.6 copy.13
  472.1 54.2 %reduce-scatter.12.cloned.1.call-done = f32[128,128]{0,1:T(8,128)} async-done(((f32[2048,128]{0,1:T(8,128)}), f32[128,128]{0,1:T(8,128)}) %reduce-scatter.12.cloned.1.call-update) | async-done | bytes 65552 | tf_op jit(solution)/shard_map/reduce_scatter | solution.py:45
  526.3 1.6 copy.12
  527.9 183.2 %reduce-scatter.6.cloned.1.call-done = f32[256,2048]{1,0:T(8,128)} async-done(((f32[4096,2048]{1,0:T(8,128)}), f32[256,2048]{1,0:T(8,128)}) %reduce-scatter.6.cloned.1.call-update) | async-done | bytes 2097168 | tf_op jit(solution)/shard_map/reduce_scatter | solution.py:40
  711.1 2.0 convolution_add_fusion.1
  713.1 2.5 fusion.26
  (19 shorter events, 0.1 us)
Async XLA Ops:
  7.2 99.5 %copy-start = (bf16[2048,1,128]{2,0,1:T(8,128)(2,1)S(1)}, bf16[2048,1,128]{2,0,1:T(8,128)(2,1)}, u32[]{:S(2)}) copy-start(bf16[2048,1,128]{2,0,1:T(8,128)(2,1)} %param.8) | copy-start | bytes 1572868
  7.2 99.5 %all-gather.7.cloned.1.call-start = ((), (), s32[]{:S(2)}) async-start(), calls=%async_computation.6 | async-start | bytes 17825792 | tf_op jit(solution)/shard_map/all_gather | solution.py:14
  8.0 134.8 %all-gather.5.cloned.1.call-start = ((), (), s32[]{:S(2)}) async-start(), calls=%async_computation.5 | async-start | bytes 1114112 | tf_op jit(solution)/shard_map/all_gather | solution.py:18
  10.5 224.4 %all-gather.11.cloned.1.call-start = ((), (), s32[]{:S(2)}) async-start(), calls=%async_computation.8 | async-start | bytes 17825792 | tf_op jit(solution)/shard_map/all_gather | solution.py:15
  11.3 263.5 %all-gather.9.cloned.1.call-start = ((), (), s32[]{:S(2)}) async-start(), calls=%async_computation.7 | async-start | bytes 1114112 | tf_op jit(solution)/shard_map/all_gather | solution.py:19
  13.9 348.8 %reduce-scatter.10.cloned.1.call-start = ((), (), s32[]{:S(2)}) async-start(), calls=%async_computation.11 | async-start | bytes 2228224 | tf_op jit(solution)/shard_map/reduce_scatter | solution.py:37
  114.9 74.2 %copy-start.8 = (bf16[4096,128]{1,0:T(8,128)(2,1)}, bf16[4096,128]{1,0:T(8,128)(2,1)S(1)}, u32[]{:S(2)}) copy-start(bf16[4096,128]{1,0:T(8,128)(2,1)S(1)} %convolution_convert_fusion.1) | copy-start | bytes 3145732
  115.0 120.0 %copy-start.7 = (bf16[1,128,2048]{2,1,0:T(8,128)(2,1)S(1)}, bf16[1,128,2048]{2,1,0:T(8,128)(2,1)}, u32[]{:S(2)}) copy-start(bf16[1,128,2048]{2,1,0:T(8,128)(2,1)} %param.11) | copy-start | bytes 1572868
  243.1 30.0 %copy-start.4 = (bf16[4096,128]{1,0:T(8,128)(2,1)}, bf16[4096,128]{1,0:T(8,128)(2,1)S(1)}, u32[]{:S(2)}) copy-start(bf16[4096,128]{1,0:T(8,128)(2,1)S(1)} %convolution_convert_fusion) | copy-start | bytes 3145732
  274.7 139.9 %reduce-scatter.8.cloned.1.call-start = ((), (), s32[]{:S(2)}) async-start(), calls=%async_computation.10 | async-start | bytes 2228224 | tf_op jit(solution)/shard_map/reduce_scatter | solution.py:36
  303.3 59.4 %copy-start.1 = (bf16[256,2048]{1,0:T(8,128)(2,1)S(1)}, bf16[256,2048]{1,0:T(8,128)(2,1)}, u32[]{:S(2)}) copy-start(bf16[256,2048]{1,0:T(8,128)(2,1)} %param.6) | copy-start | bytes 3145732
  303.3 113.7 %copy-start.3 = (bf16[4096,128]{1,0:T(8,128)(2,1)S(1)}, bf16[4096,128]{1,0:T(8,128)(2,1)}, u32[]{:S(2)}) copy-start(bf16[4096,128]{1,0:T(8,128)(2,1)} %all-gather.5.cloned.1.call-done) | copy-start | bytes 3145732
  362.6 108.0 %reduce-scatter.14.cloned.1.call-start = ((), (), s32[]{:S(2)}) async-start(), calls=%async_computation.13 | async-start | bytes 1114112 | tf_op jit(solution)/shard_map/reduce_scatter | solution.py:46
  365.0 161.3 %reduce-scatter.12.cloned.1.call-start = ((), (), s32[]{:S(2)}) async-start(), calls=%async_computation.12 | async-start | bytes 1114112 | tf_op jit(solution)/shard_map/reduce_scatter | solution.py:45
  417.0 294.1 %reduce-scatter.6.cloned.1.call-start = ((), (), s32[]{:S(2)}) async-start(), calls=%async_computation.9 | async-start | bytes 35651584 | tf_op jit(solution)/shard_map/reduce_scatter | solution.py:40
  430.1 281.0 %copy-start.2 = (bf16[2048,128]{1,0:T(8,128)(2,1)S(1)}, bf16[2048,128]{1,0:T(8,128)(2,1)}, u32[]{:S(2)}) copy-start(bf16[2048,128]{1,0:T(8,128)(2,1)} %param.9) | copy-start | bytes 1572868
  430.1 281.0 %copy-start.5 = (f32[256,128]{1,0:T(8,128)S(1)}, f32[256,128]{1,0:T(8,128)}, u32[]{:S(2)}) copy-start(f32[256,128]{1,0:T(8,128)} %reduce-scatter.8.cloned.1.call-done) | copy-start | bytes 393220
  430.1 283.0 %copy-start.6 = (f32[256,128]{1,0:T(8,128)S(1)}, f32[256,128]{1,0:T(8,128)}, u32[]{:S(2)}) copy-start(f32[256,128]{1,0:T(8,128)} %reduce-scatter.10.cloned.1.call-done) | copy-start | bytes 393220
Sparse Core Ops, SparseCore 0:
  9.7 97.0 all-gather.6
  108.9 33.7 all-gather.4
  144.4 90.4 all-gather.10
  237.0 33.7 all-gather.8
  274.8 52.1 reduce-scatter.9
  362.7 51.8 reduce-scatter.7
  417.0 53.5 reduce-scatter.13
  472.9 53.3 reduce-scatter.11
  528.7 182.3 reduce-scatter.5
where the time goes:
time: 731 us; the launch traced here: 722 us
  waiting for transfers between devices  463 us (63%)
  matrix products  216 us (30%)
  other arithmetic  21.7 us (3%)
  between operations  14.2 us (2%)
    reduce_scatter x1, waiting for transfers between devices, local_step(): dx_sum = lax.psum_scatter(dx_part, 'model', scatter_dimension=0, tiled=True)  183 us
    all_gather x1, waiting for transfers between devices, local_step(): x_full = lax.all_gather(x_loc, 'model', axis=0, tiled=True)  92.8 us
    reduce_scatter x1, waiting for transfers between devices, local_step(): lax.psum_scatter(dwk_part, 'model', scatter_dimension=0, tiled=True)  54.2 us
    reduce_scatter x1, waiting for transfers between devices, local_step(): lax.psum_scatter(dk_part, 'model', scatter_dimension=0, tiled=True)  49.6 us
    all_gather x1, waiting for transfers between devices, local_step(): dy_full = lax.all_gather(dy_loc, 'model', axis=0, tiled=True)  45.7 us
    dot_general x1, matrix products, local_step(): jnp.einsum('qhe,ke->hqk', d_attn, values_all, preferred_element_type=jnp....  42.7 us
    dot_general x1, matrix products, local_step(): jnp.einsum('hqk,qhe->ke', probs_bf, d_attn, preferred_element_type=jnp.fl...  30 us
    dot_general x1, matrix products, local_step(): jnp.einsum('hqk,ke->qhe', probs_bf, values_all, preferred_element_type=jn...  28.5 us
  transfers between devices with their start and end apart: 9, of which 7 were waited for; matrix products, arithmetic and copies ran while one was open for 33% of the time, Pallas kernels for 0%

commit v1 on v0

v1 whole, which is shorter than its diff:
```python
import math

import jax
import jax.numpy as jnp
from jax import lax
from jax.experimental import pallas as pl
from jax.experimental.pallas import tpu as pltpu
from jax.sharding import PartitionSpec as P

BF16 = jnp.bfloat16
F32 = jnp.float32
MESH = pl.DeviceIdType.MESH
RX, RY, RW, RG = range(4)


def dot(a, b):
    return jnp.dot(a, b, preferred_element_type=F32)


def dot_nt(a, b):
    return lax.dot_general(a, b, (((1,), (1,)), ((), ())), preferred_element_type=F32)


def dot_tn(a, b):
    return lax.dot_general(a, b, (((0,), (0,)), ((), ())), preferred_element_type=F32)


def rowfold(x, op):
    y = x.reshape(x.shape[0] // 8, 8, x.shape[1])
    return jnp.max(y, axis=0) if op == "max" else jnp.sum(y, axis=0)


def make_kernel(n):
    chips = n // 2
    hops = chips // 2
    last = 2 * (hops - 1)
    arrivals = last + 1

    def kernel(
        x_hbm, dy_hbm, wq_hbm, wk_hbm, wv_hbm, wo_hbm,
        dx_hbm, dwq_hbm, dwk_hbm, dwv_hbm, dwo_hbm, wq_all,
        x_all, dy_all, q_all, k_all, v_all, kt_all, vt_all, wqkv, wo,
        dkv, part, sums, gkv, dq_out, dq_in, dwqt, dwo_acc, st, wq_st,
        ot, dqt, dot_s, qt_s, do_s, dwkv, dwq_st,
        ring_r, ring_s, pair_r, pair_s, dq_r, dq_s, px_r, px_s, rs_r, rs_s, loc,
    ):
        rows, width = x_hbm.shape
        dim = wk_hbm.shape[1]
        cols = width // n
        tiles = width // rows
        scale = 1.0 / math.sqrt(dim)
        m = lax.axis_index("model")
        c = lax.div(m, 2)
        k = lax.rem(m, 2)
        mate = m + 1 - 2 * k
        nbr = (lax.rem(m + 2, n), lax.rem(m + n - 2, n))

        def remote(src, dst, ssem, rsem, dev):
            return pltpu.make_async_remote_copy(
                src_ref=src, dst_ref=dst, send_sem=ssem, recv_sem=rsem,
                device_id={"model": dev}, device_id_type=MESH,
            )

        bufs = (x_all, dy_all, wq_all, gkv)
        owns = (x_hbm, dy_hbm, wq_hbm, None)

        def half(ref, h):
            size = ref.shape[0] // 2
            return ref.at[pl.ds(pl.multiple_of(h * size, size), size), :]

        def start_own(r):
            own = gkv.at[m] if owns[r] is None else owns[r]
            for p in (0, 1):
                for d in (0, 1):
                    h = p if d == 0 else 1 - p
                    remote(half(own, h), half(bufs[r].at[m], h), ring_s.at[r, d, p], ring_r.at[r, d, p], nbr[d]).start()
            for h in (0, 1):
                remote(half(own, h), half(bufs[r].at[m], h), pair_s.at[r, h], pair_r.at[r, h], mate).start()

        def service(r, a):
            step = lax.div(a, 2) + 1
            p = lax.rem(a, 2)
            for d in (0, 1):
                blk = lax.rem(m + (n - 2 * step if d == 0 else 2 * step), n)
                chunk = half(bufs[r].at[blk], p if d == 0 else 1 - p)
                remote(chunk, chunk, ring_s.at[r, d, 0], ring_r.at[r, d, a], nbr[d]).wait_recv()

                @pl.when(a <= last - 2)
                def _():
                    remote(chunk, chunk, ring_s.at[r, d, 2 + a], ring_r.at[r, d, a + 2], nbr[d]).start()

                i = 2 + d * arrivals + a
                remote(chunk, chunk, pair_s.at[r, i], pair_r.at[r, i], mate).start()

        def chip_at(u):
            step = lax.div(u + 1, 2)
            odd = lax.rem(u, 2)
            return lax.rem(c + odd * (chips - step) + (1 - odd) * step, chips)

        def wait_pair(r, u):
            blk = bufs[r].at[2 * chip_at(u) + 1 - k]

            def wait(h, i):
                chunk = half(blk, h)
                remote(chunk, chunk, pair_s.at[r, 0], pair_r.at[r, i], mate).wait_recv()

            @pl.when(u == 0)
            def _():
                wait(0, 0)
                wait(1, 1)

            @pl.when(u > 0)
            def _():
                d = 1 - lax.rem(u, 2)
                i = 2 + d * arrivals + 2 * (lax.div(u + 1, 2) - 1)
                wait(d, i)
                wait(1 - d, i + 1 + lax.div(u, chips - 1) * last)

        def wait_sends(r):
            own = gkv.at[m] if owns[r] is None else owns[r]
            chunk = half(own, 0)
            for d in (0, 1):
                for i in range(last + 1):
                    remote(chunk, chunk, ring_s.at[r, d, i], ring_r.at[r, d, 0], nbr[d]).wait_send()
            for i in range(2 + 2 * arrivals):
                remote(chunk, chunk, pair_s.at[r, i], pair_r.at[r, 0], mate).wait_send()

        def local(src, dst, i):
            return pltpu.make_async_copy(src, dst, loc.at[i])

        loads = [
            local(x_hbm, x_all.at[m], 0),
            local(wq_hbm, wqkv.at[:, pl.ds(0, dim)], 1),
            local(wk_hbm, wqkv.at[:, pl.ds(dim, dim)], 2),
            local(wv_hbm, wqkv.at[:, pl.ds(2 * dim, dim)], 3),
            local(wo_hbm, wo, 4),
            local(dy_hbm, dy_all.at[m], 5),
        ]
        for load in loads:
            load.start()
        barrier = pltpu.get_barrier_semaphore()
        for i in range(1, n):
            pl.semaphore_signal(barrier, inc=1, device_id={"model": lax.rem(m + i, n)}, device_id_type=MESH)
        pl.semaphore_wait(barrier, n - 1)
        start_own(RX)
        dwqt[...] = jnp.zeros_like(dwqt)
        dwo_acc[...] = jnp.zeros_like(dwo_acc)
        dwkv[...] = jnp.zeros_like(dwkv)

        def clear(j, _):
            dkv[j] = jnp.zeros(dkv.shape[1:], F32)
            return 0

        lax.fori_loop(0, n, clear, 0)
        for load in loads:
            load.wait()

        def project(blk):
            qkv = dot(x_all[blk], wqkv[...]).astype(BF16)
            q_all[blk] = qkv[:, :dim]
            k_all[blk] = qkv[:, dim : 2 * dim]
            v_all[blk] = qkv[:, 2 * dim :]
            kt_all[blk] = qkv[:, dim : 2 * dim].T
            vt_all[blk] = qkv[:, 2 * dim :].T

        def steps(r, follow, work, extra=None):
            def body(v, _):
                u = lax.div(v, 2)
                kk = lax.rem(v, 2)

                @pl.when(v == 2)
                def _():
                    service(r, 0)

                @pl.when((kk == 0) & (u >= 1) & (u <= last))
                def _():
                    service(r, u)

                @pl.when(v == 2 * (last - 2))
                def _():
                    start_own(follow)

                @pl.when(kk == 1)
                def _():
                    wait_pair(r, u)

                if extra is not None:
                    extra(v)
                work(2 * chip_at(u) + lax.rem(k + kk, 2))
                return 0

            lax.fori_loop(0, n, body, 0)

        steps(RX, RY, project)

        def attend(blk):
            q = q_all[blk]
            do = dot_nt(dy_all[blk], wo[...]).astype(BF16)
            do_s[...] = do
            dot_s[...] = do.T
            qt_s[...] = q.T

            def scores(j, top):
                s = dot(k_all[j], qt_s[...])
                st[j] = s
                return jnp.maximum(top, rowfold(s, "max"))

            top = lax.fori_loop(0, blk, scores, jnp.full((8, rows), -jnp.inf, F32))
            s = dot(k_all[blk], qt_s[...])
            key = lax.broadcasted_iota(jnp.int32, (rows, rows), 0)
            query = lax.broadcasted_iota(jnp.int32, (rows, rows), 1)
            s = jnp.where(key <= query, s, -jnp.inf)
            st[blk] = s
            top = jnp.max(jnp.maximum(top, rowfold(s, "max")), axis=0, keepdims=True)
            factor = scale * math.log2(math.e)

            def weights(j, total):
                p = jnp.exp2((st[j] - top) * factor)
                st[j] = p
                return total + rowfold(p, "sum")

            total = lax.fori_loop(0, blk + 1, weights, jnp.zeros((8, rows), F32))
            inv = 1.0 / jnp.sum(total, axis=0, keepdims=True)
            ot[...] = jnp.zeros_like(ot)
            dqt[...] = jnp.zeros_like(dqt)

            def outputs(j, _):
                p = (st[j] * inv).astype(BF16)
                ot[...] += dot(vt_all[j], p)
                dkv[j, 1] += dot(p, do_s[...])
                return 0

            lax.fori_loop(0, blk + 1, outputs, 0)
            o = ot[...].astype(BF16)
            row = jnp.sum(dot_s[...].astype(F32) * o.astype(F32), axis=0, keepdims=True)

            def grads(j, _):
                dp = dot(v_all[j], dot_s[...])
                g = ((st[j] * inv) * (dp - row) * scale).astype(BF16)
                dqt[...] += dot(kt_all[j], g)
                dkv[j, 0] += dot(g, q_all[blk])
                return 0

            lax.fori_loop(0, blk + 1, grads, 0)
            dq = dqt[...].astype(BF16)
            dq_out[blk] = dq.T

            @pl.when(blk != m)
            def _():
                remote(dq_out.at[blk], dq_in.at[m], dq_s.at[blk], dq_r.at[m], blk).start()

            for t in range(tiles):
                at = pl.ds(t * rows, rows)
                dwqt[:, at] += dot(dq, x_all[blk, :, at])
                dwo_acc[:, at] += dot(o, dy_all[blk, :, at])

        def extra(v):
            @pl.when(v == n - 2)
            def _():
                service(RW, 0)

            @pl.when(v == n - 1)
            def _():
                service(RW, 1)

        steps(RY, RW, attend, extra)

        order = [hops]
        for step in range(hops - 1, 0, -1):
            order += [step, -step]
        order.append(0)

        def chip_off(off):
            return lax.rem(c + off + chips, chips)

        def px(i):
            chip = chip_off(order[i])
            return remote(dkv.at[2 * chip + 1 - k], part.at[chip], px_s.at[i], px_r.at[i], mate)

        for i in range(chips):
            px(i).start()
        dwo_out = local(dwo_acc, dwo_hbm, 0)
        dwo_out.start()
        for t in range(tiles):
            at = pl.ds(t * rows, rows)
            dwq_st[at, :] = dwqt[:, at].T
            st[t] = jnp.zeros((rows, rows), F32)
        dwq_out = local(dwq_st, dwq_hbm, 1)
        dwq_out.start()

        def add_dx(dq, w_ref):
            for t in range(tiles):
                st[t] += dot_nt(dq, w_ref[pl.ds(t * rows, rows), :])

        def dx_heads(lo, hi):
            def body(v, _):
                u = lax.div(v, 2)
                kk = lax.rem(v, 2)
                h = 2 * chip_at(u) + lax.rem(k + kk, 2)

                @pl.when(kk == 1)
                def _():
                    wait_pair(RW, u)

                fetch = local(wq_all.at[h], wq_st.at[0], 2)
                fetch.start()
                remote(dq_in.at[h], dq_in.at[h], dq_s.at[h], dq_r.at[h], mate).wait_recv()
                fetch.wait()
                add_dx(dq_in[h], wq_st.at[0])
                return 0

            lax.fori_loop(lo, hi, body, 0)

        def gather(i):
            px(i).wait_recv()
            chip = chip_off(order[i])
            part[chip] += dkv[2 * chip + k]

        def rs(d, t, h, src):
            return remote(src, sums.at[d, t - 1, h], rs_s.at[d, t - 1, h], rs_r.at[d, t - 1, h], nbr[d])

        sent = []

        def hop(t):
            for d in (0, 1):
                chip = chip_off((hops + 1 - t) * (1 - 2 * d))
                for h in (d, 1 - d):
                    if t == 1 and h != d:
                        continue
                    if t == 1 or (t == 2 and h != d):
                        copy = rs(d, t, h, part.at[chip, h])
                    else:
                        held = sums.at[d, t - 2, h]
                        rs(d, t - 1, h, held).wait_recv()
                        held[...] += part[chip, h]
                        copy = rs(d, t, h, held)
                    copy.start()
                    sent.append(copy)

        service(RW, 2)
        gather(0)
        hop(1)
        service(RW, 3)
        gather(1)
        gather(2)
        hop(2)
        add_dx(dq_out[m], wqkv.at[:, pl.ds(0, dim)])
        dx_heads(1, 2)
        for i in range(3, chips):
            gather(i)
        done = 2
        for t in range(3, hops + 1):
            hop(t)
            service(RW, t + 1)
            dx_heads(done, done + 4)
            done += 4
        for t in range(hops + 2, last + 1):
            service(RW, t)
        for h in (0, 1):
            total = part[c, h]
            for d in (0, 1):
                held = sums.at[d, hops - 1, h]
                rs(d, hops, h, held).wait_recv()
                total += held[...]
            gkv[m, :, pl.ds(h * dim, dim)] = total.astype(BF16)
        start_own(RG)
        for t in range(tiles):
            at = pl.ds(t * rows, rows)
            st[t] += dot_nt(gkv[m], wqkv[at, pl.ds(dim, 2 * dim)])
        dx_heads(done, n)
        wait_sends(RY)
        for t in range(tiles):
            dy_all[0, :, pl.ds(t * rows, rows)] = st[t].astype(BF16)
        dx_out = local(dy_all.at[0], dx_hbm, 2)
        dx_out.start()

        def key_grads(blk):
            xs = x_all[blk, :, pl.ds(pl.multiple_of(m * cols, cols), cols)]
            dwkv[...] += dot_tn(xs, gkv[blk])

        def last_steps(v, _):
            u = lax.div(v, 2)
            kk = lax.rem(v, 2)

            @pl.when(v == 2)
            def _():
                service(RG, 0)

            @pl.when((kk == 0) & (u >= 1) & (u <= last))
            def _():
                service(RG, u)

            @pl.when(kk == 1)
            def _():
                wait_pair(RG, u)

            key_grads(2 * chip_at(u) + lax.rem(k + kk, 2))
            return 0

        lax.fori_loop(0, n, last_steps, 0)
        outs = [
            local(dwkv.at[:, pl.ds(0, dim)], dwk_hbm, 3),
            local(dwkv.at[:, pl.ds(dim, dim)], dwv_hbm, 4),
        ]
        for out in outs:
            out.start()
        for out in (dwo_out, dwq_out, dx_out, *outs):
            out.wait()

        for r in (RX, RW, RG):
            wait_sends(r)
        for i in range(chips):
            px(i).wait_send()
        for copy in sent:
            copy.wait_send()

        def sent_dq(h, _):
            @pl.when(h != m)
            def _():
                remote(dq_out.at[h], dq_in.at[h], dq_s.at[h], dq_r.at[h], h).wait_send()

            return 0

        lax.fori_loop(0, n, sent_dq, 0)

    return kernel


def solution(mesh):
    n = mesh.shape["model"]
    chips = n // 2
    hops = chips // 2
    tok_spec = P(("data", "model"), None)

    def local_step(x_loc, dy_loc, wq_loc, w_key, w_value, wo_loc):
        rows, width = x_loc.shape
        dim = w_key.shape[1]
        cols = width // n
        sds = jax.ShapeDtypeStruct
        vmem = pltpu.VMEM
        dma = pltpu.SemaphoreType.DMA
        arrivals = 2 * hops - 1
        outs = pl.pallas_call(
            make_kernel(n),
            name="mqa_backward",
            out_shape=(
                sds((rows, width), BF16),
                sds((width, dim), F32),
                sds((cols, dim), F32),
                sds((cols, dim), F32),
                sds((dim, width), F32),
                sds((n, width, dim), BF16),
            ),
            in_specs=[pl.BlockSpec(memory_space=pl.ANY)] * 6,
            out_specs=[pl.BlockSpec(memory_space=pl.ANY)] * 6,
            scratch_shapes=[
                vmem((n, rows, width), BF16),
                vmem((n, rows, width), BF16),
                vmem((n, rows, dim), BF16),
                vmem((n, rows, dim), BF16),
                vmem((n, rows, dim), BF16),
                vmem((n, dim, rows), BF16),
                vmem((n, dim, rows), BF16),
                vmem((width, 3 * dim), BF16),
                vmem((dim, width), BF16),
                vmem((n, 2, rows, dim), F32),
                vmem((chips, 2, rows, dim), F32),
                vmem((2, hops, 2, rows, dim), F32),
                vmem((n, rows, 2 * dim), BF16),
                vmem((n, rows, dim), BF16),
                vmem((n, rows, dim), BF16),
                vmem((dim, width), F32),
                vmem((dim, width), F32),
                vmem((n, rows, rows), F32),
                vmem((1, width, dim), BF16),
                vmem((dim, rows), F32),
                vmem((dim, rows), F32),
                vmem((dim, rows), BF16),
                vmem((dim, rows), BF16),
                vmem((rows, dim), BF16),
                vmem((cols, 2 * dim), F32),
                vmem((width, dim), F32),
                dma((4, 2, arrivals)),
                dma((4, 2, arrivals)),
                dma((4, 2 + 2 * arrivals)),
                dma((4, 2 + 2 * arrivals)),
                dma((n,)),
                dma((n,)),
                dma((chips,)),
                dma((chips,)),
                dma((2, hops, 2)),
                dma((2, hops, 2)),
                dma((6,)),
            ],
            compiler_params=pltpu.CompilerParams(
                collective_id=0, has_side_effects=True, vmem_limit_bytes=67043328
            ),
        )(
            x_loc,
            dy_loc,
            wq_loc.reshape(width, dim),
            w_key,
            w_value,
            wo_loc.reshape(dim, width),
        )
        dx, dwq, dwk, dwv, dwo, _ = outs
        return dx, dwq.reshape(width, 1, dim), dwk, dwv, dwo.reshape(1, dim, width)

    return jax.shard_map(
        local_step,
        mesh=mesh,
        in_specs=(tok_spec, tok_spec, P(None, "model", None), P(None, None), P(None, None), P("model", None, None)),
        out_specs=(tok_spec, P("data", "model", None), tok_spec, tok_spec, P(("data", "model"), None, None)),
        check_vma=False,
    )
```

time: 731 us -> 319 us (0.44); the launches traced: 722 us -> 318 us
  waiting for transfers between devices: 463 us -> 0 us
  Pallas kernels: 0 us -> 308 us
  matrix products: 216 us -> 0 us
  other arithmetic: 21.7 us -> 0 us
  between operations: 14.2 us -> 0.64 us
    pallas_call x0 -> x1, Pallas kernels: none -> 308 us  [local_step(): pl.pallas_call(make_kernel(n), name='mqa_backward', out_shape=(sds((rows,...]
    reduce_scatter x5 -> x0, waiting for transfers between devices: 295 us -> none  [the longest x1 183 us: local_step(): dx_sum = lax.psum_scatter(dx_part, 'model', scatter_dimension=0, tiled=True)]
    dot_general x17 -> x0, matrix products: 216 us -> none  [the longest x1 42.7 us: local_step(): jnp.einsum('qhe,ke->hqk', d_attn, values_all, preferred_element_type=jnp....]
    all_gather x4 -> x0, waiting for transfers between devices: 166 us -> none  [the longest x1 92.8 us: local_step(): x_full = lax.all_gather(x_loc, 'model', axis=0, tiled=True)]
    reduce_sum x1 -> x0, other arithmetic: 21.7 us -> none  [local_step(): probs_f32 = jax.nn.softmax(scores, axis=-1)]
  transfers between devices with their start and end apart: 9 -> 0, of which waited for: 7 -> 0; matrix products, arithmetic and copies ran while one was open for 33% -> 0% of each run, Pallas kernels for 0% -> 0%
where the time goes in v1:
time: 319 us; the launch traced here: 318 us
  Pallas kernels  308 us (97%)
  local copies, waits for them, and re-layouts  9.58 us (3%)
    pallas_call x1, Pallas kernels, local_step(): pl.pallas_call(make_kernel(n), name='mqa_backward', out_shape=(sds((rows,...  308 us
    unnamed x5, local copies, waits for them, and re-layouts  9.58 us

profile of v1, /device:TPU:21, one launch (start us, length us, event | category | flops | bytes accessed | tf_op | source)
XLA Modules:
  0.0 318.2 jit_solution(16612424039735043809)
XLA Ops:
  0.6 308.0 %mqa_backward.1 = (bf16[256,2048]{1,0:T(8,128)(2,1)}, f32[2048,128]{1,0:T(8,128)}, f32[128,128]{1,0:T(8,128)}, f32[128,128]{1,0:T(8,128)}, f32[128,2048]{1,0:T(8,128)}, /*index=5*/bf16[16,2048,128]{2,1,0:T(8,128)(2,1)}) custom-call(bf16[256,2048]{1,0:T(8,128)(2,1)} %x_hbm.1, bf16[256,2048]{1,0:T(8,128)(2,1)} %dy_hbm.1, bf16[2048,128]{1,0:T(8,128)(2,1)} %bitcast.8, ...), custom_call_target="tpu_custom_call" | custom-call | tf_op jit(solution)/shard_map/mqa_backward/pallas_call | solution.py:443
  308.6 2.3 copy.17
  310.9 2.0 copy.18
  313.0 1.5 copy.19
  314.4 1.5 copy.20
  315.9 2.3 copy.21

commit v2 on v1

v2 whole, which is shorter than its diff:
```python
import math

import jax
import jax.numpy as jnp
from jax import lax
from jax.experimental import pallas as pl
from jax.experimental.pallas import tpu as pltpu
from jax.sharding import PartitionSpec as P

BF16 = jnp.bfloat16
F32 = jnp.float32
MESH = pl.DeviceIdType.MESH
RX, RY, RW, RG = range(4)


def dot(a, b):
    return jnp.dot(a, b, preferred_element_type=F32)


def dot_nt(a, b):
    return lax.dot_general(a, b, (((1,), (1,)), ((), ())), preferred_element_type=F32)


def dot_tn(a, b):
    return lax.dot_general(a, b, (((0,), (0,)), ((), ())), preferred_element_type=F32)


def rowfold(x, op):
    y = x.reshape(x.shape[0] // 8, 8, x.shape[1])
    return jnp.max(y, axis=0) if op == "max" else jnp.sum(y, axis=0)


def make_kernel(n):
    chips = n // 2
    hops = chips // 2
    last = 2 * (hops - 1)
    arrivals = last + 1

    def kernel(
        x_hbm, dy_hbm, wq_hbm, wk_hbm, wv_hbm, wo_hbm,
        dx_hbm, dwq_hbm, dwk_hbm, dwv_hbm, dwo_hbm, wq_all,
        x_all, dy_all, q_all, kv_all, kt_all, vt_all, wqkv, wo,
        dkv, part, sums, dq_in, dwqt, dwo_acc, st, wq_st,
        ot, dqt, dot_s, qt_s, do_s, dwkv,
        ring_r, ring_s, pair_r, pair_s, dq_r, dq_s, px_r, px_s, rs_r, rs_s, loc,
    ):
        rows, width = x_hbm.shape
        dim = wk_hbm.shape[1]
        cols = width // n
        tiles = width // rows
        scale = 1.0 / math.sqrt(dim)
        m = lax.axis_index("model")
        c = lax.div(m, 2)
        k = lax.rem(m, 2)
        mate = m + 1 - 2 * k
        nbr = (lax.rem(m + 2, n), lax.rem(m + n - 2, n))

        def remote(src, dst, ssem, rsem, dev):
            return pltpu.make_async_remote_copy(
                src_ref=src, dst_ref=dst, send_sem=ssem, recv_sem=rsem,
                device_id={"model": dev}, device_id_type=MESH,
            )

        bufs = (x_all, dy_all, wq_all)
        owns = (x_hbm, dy_hbm, wq_hbm)

        def half(ref, h):
            size = ref.shape[0] // 2
            return ref.at[pl.ds(pl.multiple_of(h * size, size), size), :]

        def chunk_at(r, blk, h):
            if r == RG:
                at = pl.ds(pl.multiple_of(lax.rem(blk, 2) * rows, rows), rows)
                return kv_all.at[h, lax.div(blk, 2), at, :]
            return half(bufs[r].at[blk], h)

        def own_at(r, h):
            return chunk_at(r, m, h) if r == RG else half(owns[r], h)

        def start_own(r):
            for p in (0, 1):
                for d in (0, 1):
                    h = p if d == 0 else 1 - p
                    remote(own_at(r, h), chunk_at(r, m, h), ring_s.at[r, d, p], ring_r.at[r, d, p], nbr[d]).start()
            for h in (0, 1):
                remote(own_at(r, h), chunk_at(r, m, h), pair_s.at[r, h], pair_r.at[r, h], mate).start()

        def service(r, a):
            step = lax.div(a, 2) + 1
            p = lax.rem(a, 2)
            for d in (0, 1):
                blk = lax.rem(m + (n - 2 * step if d == 0 else 2 * step), n)
                chunk = chunk_at(r, blk, p if d == 0 else 1 - p)
                remote(chunk, chunk, ring_s.at[r, d, 0], ring_r.at[r, d, a], nbr[d]).wait_recv()

                @pl.when(a <= last - 2)
                def _():
                    remote(chunk, chunk, ring_s.at[r, d, 2 + a], ring_r.at[r, d, a + 2], nbr[d]).start()

                i = 2 + d * arrivals + a
                remote(chunk, chunk, pair_s.at[r, i], pair_r.at[r, i], mate).start()

        def chip_at(u):
            step = lax.div(u + 1, 2)
            odd = lax.rem(u, 2)
            return lax.rem(c + odd * (chips - step) + (1 - odd) * step, chips)

        def wait_pair(r, u):
            blk = 2 * chip_at(u) + 1 - k

            def wait(h, i):
                chunk = chunk_at(r, blk, h)
                remote(chunk, chunk, pair_s.at[r, 0], pair_r.at[r, i], mate).wait_recv()

            @pl.when(u == 0)
            def _():
                wait(0, 0)
                wait(1, 1)

            @pl.when(u > 0)
            def _():
                d = 1 - lax.rem(u, 2)
                i = 2 + d * arrivals + 2 * (lax.div(u + 1, 2) - 1)
                wait(d, i)
                wait(1 - d, i + 1 + lax.div(u, chips - 1) * last)

        def wait_sends(r):
            chunk = own_at(r, 0)
            for d in (0, 1):
                for i in range(last + 1):
                    remote(chunk, chunk, ring_s.at[r, d, i], ring_r.at[r, d, 0], nbr[d]).wait_send()
            for i in range(2 + 2 * arrivals):
                remote(chunk, chunk, pair_s.at[r, i], pair_r.at[r, 0], mate).wait_send()

        def local(src, dst, i):
            return pltpu.make_async_copy(src, dst, loc.at[i])

        loads = [
            local(x_hbm, x_all.at[m], 0),
            local(wq_hbm, wqkv.at[:, pl.ds(0, dim)], 1),
            local(wk_hbm, wqkv.at[:, pl.ds(dim, dim)], 2),
            local(wv_hbm, wqkv.at[:, pl.ds(2 * dim, dim)], 3),
            local(wo_hbm, wo, 4),
            local(dy_hbm, dy_all.at[m], 5),
        ]
        for load in loads:
            load.start()
        barrier = pltpu.get_barrier_semaphore()
        for i in range(1, n):
            pl.semaphore_signal(barrier, inc=1, device_id={"model": lax.rem(m + i, n)}, device_id_type=MESH)
        pl.semaphore_wait(barrier, n - 1)
        start_own(RX)
        dwqt[...] = jnp.zeros_like(dwqt)
        dwo_acc[...] = jnp.zeros_like(dwo_acc)
        dwkv[...] = jnp.zeros_like(dwkv)

        def clear(j, _):
            dkv[j] = jnp.zeros(dkv.shape[1:], F32)
            return 0

        lax.fori_loop(0, n, clear, 0)
        for load in loads:
            load.wait()

        def project(ch):
            for i in (0, 1):
                at = pl.ds(i * rows, rows)
                qkv = dot(x_all[2 * ch + i], wqkv[...]).astype(BF16)
                q_all[ch, at, :] = qkv[:, :dim]
                kv_all[0, ch, at, :] = qkv[:, dim : 2 * dim]
                kv_all[1, ch, at, :] = qkv[:, 2 * dim :]
                kt_all[ch, :, at] = qkv[:, dim : 2 * dim].T
                vt_all[ch, :, at] = qkv[:, 2 * dim :].T

        def gathered(u, _):
            @pl.when(u == 1)
            def _():
                service(RX, 0)

            @pl.when((u >= 1) & (u <= last))
            def _():
                service(RX, u)

            @pl.when(u == last - 2)
            def _():
                start_own(RW)

            @pl.when(u == last)
            def _():
                start_own(RY)

            wait_pair(RX, u)
            project(chip_at(u))
            return 0

        lax.fori_loop(0, chips, gathered, 0)

        pair = 2 * rows
        factor = scale * math.log2(math.e)
        halves = [pl.ds(i * rows, rows) for i in (0, 1)]

        def attend(ch):
            for i in (0, 1):
                do_s[halves[i], :] = dot_nt(dy_all[2 * ch + i], wo[...]).astype(BF16)
            dot_s[...] = do_s[...].T
            qt_s[...] = q_all[ch].T

            def scores(j, top):
                for at in halves:
                    s = dot(kv_all[0, j, at, :], qt_s[...])
                    st[j, at, :] = s
                    top = jnp.maximum(top, rowfold(s, "max"))
                return top

            top = lax.fori_loop(0, ch, scores, jnp.full((8, pair), -jnp.inf, F32))
            for i in (0, 1):
                s = dot(kv_all[0, ch, halves[i], :], qt_s[...])
                key = lax.broadcasted_iota(jnp.int32, (rows, pair), 0) + i * rows
                query = lax.broadcasted_iota(jnp.int32, (rows, pair), 1)
                s = jnp.where(key <= query, s, -jnp.inf)
                st[ch, halves[i], :] = s
                top = jnp.maximum(top, rowfold(s, "max"))
            top = jnp.max(top, axis=0, keepdims=True)

            def weights(j, total):
                for at in halves:
                    p = jnp.exp2((st[j, at, :] - top) * factor)
                    st[j, at, :] = p
                    total += rowfold(p, "sum")
                return total

            total = lax.fori_loop(0, ch + 1, weights, jnp.zeros((8, pair), F32))
            inv = 1.0 / jnp.sum(total, axis=0, keepdims=True)
            ot[...] = jnp.zeros_like(ot)
            dqt[...] = jnp.zeros_like(dqt)

            def outputs(j, _):
                p = (st[j] * inv).astype(BF16)
                ot[...] += dot(vt_all[j], p)
                dv = dot(p, do_s[...])
                for i in (0, 1):
                    dkv[2 * j + i, 1] += dv[i * rows : (i + 1) * rows]
                return 0

            lax.fori_loop(0, ch + 1, outputs, 0)
            o = ot[...].astype(BF16)
            row = jnp.sum(dot_s[...].astype(F32) * o.astype(F32), axis=0, keepdims=True)
            inv_scale = inv * scale

            def grads(j, _):
                dp = dot(kv_all[1, j], dot_s[...])
                g = ((st[j] * inv_scale) * (dp - row)).astype(BF16)
                dqt[...] += dot(kt_all[j], g)
                dk = dot(g, q_all[ch])
                for i in (0, 1):
                    dkv[2 * j + i, 0] += dk[i * rows : (i + 1) * rows]
                return 0

            lax.fori_loop(0, ch + 1, grads, 0)
            dq = dqt[...].astype(BF16)
            q_all[ch] = dq.T
            for i in (0, 1):
                blk = 2 * ch + i

                @pl.when(blk != m)
                def _():
                    remote(q_all.at[ch, halves[i], :], dq_in.at[m], dq_s.at[blk], dq_r.at[m], blk).start()

            for t in range(tiles):
                at = pl.ds(t * rows, rows)
                add_q = dot(dq[:, :rows], x_all[2 * ch, :, at])
                add_o = dot(o[:, :rows], dy_all[2 * ch, :, at])
                dwqt[:, at] += add_q + dot(dq[:, rows:], x_all[2 * ch + 1, :, at])
                dwo_acc[:, at] += add_o + dot(o[:, rows:], dy_all[2 * ch + 1, :, at])

        def attended(u, _):
            @pl.when(u == 1)
            def _():
                for a in range(1, last - 3):
                    service(RW, a)
                service(RY, 0)

            @pl.when((u >= 1) & (u <= last))
            def _():
                service(RY, u)

            @pl.when(u == last - 2)
            def _():
                service(RW, last - 3)
                service(RW, last - 2)

            wait_pair(RY, u)
            attend(chip_at(u))
            return 0

        service(RW, 0)
        lax.fori_loop(0, chips, attended, 0)

        order = [hops]
        for step in range(hops - 1, 0, -1):
            order += [step, -step]
        order.append(0)

        def chip_off(off):
            return lax.rem(c + off + chips, chips)

        def px(i):
            chip = chip_off(order[i])
            return remote(dkv.at[2 * chip + 1 - k], part.at[chip], px_s.at[i], px_r.at[i], mate)

        for i in range(chips):
            px(i).start()
        dwo_out = local(dwo_acc, dwo_hbm, 0)
        dwo_out.start()
        spare = width // pair
        dwq_out = []
        for t in range(spare):
            at = pl.ds(t * pair, pair)
            staged = st.at[spare + t, :, pl.ds(0, dim)]
            staged[...] = dwqt[:, at].T
            out = local(staged, dwq_hbm.at[at, :], 6 + t)
            out.start()
            dwq_out.append(out)
            st[t, pl.ds(0, rows), :] = jnp.zeros((rows, pair), F32)

        def add_dx(dq, w_ref):
            for t in range(spare):
                st[t, pl.ds(0, rows), :] += dot_nt(dq, w_ref[pl.ds(t * pair, pair), :])

        def head_at(v):
            return 2 * chip_at(lax.div(v, 2)) + lax.rem(k + lax.rem(v, 2), 2)

        def fetch(v):
            slot = lax.rem(v, 2)
            return local(wq_all.at[head_at(v)], wq_st.at[slot], 2 + slot)

        def dx_head(v):
            h = head_at(v)
            fetch(v).wait()
            remote(dq_in.at[h], dq_in.at[h], dq_s.at[h], dq_r.at[h], mate).wait_recv()
            add_dx(dq_in[h], wq_st.at[lax.rem(v, 2)])

        def dx_heads(lo, hi):
            def body(v, _):
                @pl.when(lax.rem(v, 2) == 1)
                def _():
                    wait_pair(RW, lax.div(v, 2))

                fetch(v).start()

                @pl.when(v > 1)
                def _():
                    dx_head(v - 1)

                return 0

            lax.fori_loop(lo, hi, body, 0)

        def gather(i):
            px(i).wait_recv()
            chip = chip_off(order[i])
            part[chip] += dkv[2 * chip + k]

        def rs(d, t, h, src):
            return remote(src, sums.at[d, t - 1, h], rs_s.at[d, t - 1, h], rs_r.at[d, t - 1, h], nbr[d])

        sent = []

        def hop(t):
            for d in (0, 1):
                chip = chip_off((hops + 1 - t) * (1 - 2 * d))
                for h in (d, 1 - d):
                    if t == 1 and h != d:
                        continue
                    if t == 1 or (t == 2 and h != d):
                        copy = rs(d, t, h, part.at[chip, h])
                    else:
                        held = sums.at[d, t - 2, h]
                        rs(d, t - 1, h, held).wait_recv()
                        held[...] += part[chip, h]
                        copy = rs(d, t, h, held)
                    copy.start()
                    sent.append(copy)

        gather(0)
        hop(1)
        add_dx(q_all[c, pl.ds(pl.multiple_of(k * rows, rows), rows), :], wqkv.at[:, pl.ds(0, dim)])
        dx_heads(1, 3)
        gather(1)
        gather(2)
        hop(2)
        dx_heads(3, 5)
        for i in range(3, chips):
            gather(i)
        done = 5
        for t in range(3, hops + 1):
            hop(t)
            service(RW, last - hops + t)
            dx_heads(done, done + 4)
            done += 4

        def turn(j, _):
            for i in (0, 1):
                xs = x_all[2 * j + i, :, pl.ds(pl.multiple_of(m * cols, cols), cols)]
                kt_all[j, pl.ds(0, cols), halves[i]] = xs.T
            return 0

        lax.fori_loop(0, chips, turn, 0)
        for h in (0, 1):
            total = part[c, h]
            for d in (0, 1):
                held = sums.at[d, hops - 1, h]
                rs(d, hops, h, held).wait_recv()
                total += held[...]
            chunk_at(RG, m, h)[...] = total.astype(BF16)
        start_own(RG)
        own_kv = [chunk_at(RG, m, h)[...] for h in (0, 1)]
        for t in range(spare):
            at = pl.ds(t * pair, pair)
            add = dot_nt(own_kv[0], wqkv[at, pl.ds(dim, dim)])
            add += dot_nt(own_kv[1], wqkv[at, pl.ds(2 * dim, dim)])
            st[t, pl.ds(0, rows), :] += add
        dx_heads(done, n)
        dx_head(n - 1)
        wait_sends(RY)
        for t in range(spare):
            dy_all[0, :, pl.ds(t * pair, pair)] = st[t, pl.ds(0, rows), :].astype(BF16)
        dx_out = local(dy_all.at[0], dx_hbm, 4)
        dx_out.start()

        def last_steps(u, _):
            @pl.when(u == 1)
            def _():
                service(RG, 0)

            @pl.when((u >= 1) & (u <= last))
            def _():
                service(RG, u)

            wait_pair(RG, u)
            ch = chip_at(u)
            for h in (0, 1):
                dwkv[h] += dot(kt_all[ch, pl.ds(0, cols), :], kv_all[h, ch])
            return 0

        lax.fori_loop(0, chips, last_steps, 0)
        outs = [
            local(dwkv.at[0], dwk_hbm, 2),
            local(dwkv.at[1], dwv_hbm, 3),
        ]
        for out in outs:
            out.start()
        for out in (dwo_out, *dwq_out, dx_out, *outs):
            out.wait()

        for r in (RX, RW, RG):
            wait_sends(r)
        for i in range(chips):
            px(i).wait_send()
        for copy in sent:
            copy.wait_send()

        def sent_dq(h, _):
            @pl.when(h != m)
            def _():
                remote(dq_in.at[h], dq_in.at[h], dq_s.at[h], dq_r.at[h], h).wait_send()

            return 0

        lax.fori_loop(0, n, sent_dq, 0)

    return kernel


def hand_on(*refs):
    count = (len(refs) - 2) // 3
    srcs, dsts, bufs = refs[:count], refs[count : 2 * count], refs[2 * count : 3 * count]
    sems_in, sems_out = refs[3 * count :]
    pieces = []
    for src, dst, buf in zip(srcs, dsts, bufs):
        parts = max(1, src.shape[0] * src.shape[1] // (1 << 16))
        size = src.shape[0] // parts
        for i in range(parts):
            at = pl.ds(i * size, size)
            pieces.append((src.at[at, :], buf.at[at, :], dst.at[at, :]))
    ins = [pltpu.make_async_copy(a, b, sems_in.at[i]) for i, (a, b, _) in enumerate(pieces)]
    outs = [pltpu.make_async_copy(b, c, sems_out.at[i]) for i, (_, b, c) in enumerate(pieces)]
    for copy in ins:
        copy.start()
    for got, put in zip(ins, outs):
        got.wait()
        put.start()
    for put in outs:
        put.wait()


def solution(mesh):
    n = mesh.shape["model"]
    chips = n // 2
    hops = chips // 2
    tok_spec = P(("data", "model"), None)

    def local_step(x_loc, dy_loc, wq_loc, w_key, w_value, wo_loc):
        rows, width = x_loc.shape
        dim = w_key.shape[1]
        cols = width // n
        sds = jax.ShapeDtypeStruct
        vmem = pltpu.VMEM
        dma = pltpu.SemaphoreType.DMA
        arrivals = 2 * hops - 1
        outs = pl.pallas_call(
            make_kernel(n),
            name="mqa_backward",
            out_shape=(
                sds((rows, width), BF16),
                sds((width, dim), F32),
                sds((cols, dim), F32),
                sds((cols, dim), F32),
                sds((dim, width), F32),
                sds((n, width, dim), BF16),
            ),
            in_specs=[pl.BlockSpec(memory_space=pl.ANY)] * 6,
            out_specs=[pl.BlockSpec(memory_space=pl.ANY)] * 6,
            scratch_shapes=[
                vmem((n, rows, width), BF16),
                vmem((n, rows, width), BF16),
                vmem((chips, 2 * rows, dim), BF16),
                vmem((2, chips, 2 * rows, dim), BF16),
                vmem((chips, dim, 2 * rows), BF16),
                vmem((chips, dim, 2 * rows), BF16),
                vmem((width, 3 * dim), BF16),
                vmem((dim, width), BF16),
                vmem((n, 2, rows, dim), F32),
                vmem((chips, 2, rows, dim), F32),
                vmem((2, hops, 2, rows, dim), F32),
                vmem((n, rows, dim), BF16),
                vmem((dim, width), F32),
                vmem((dim, width), F32),
                vmem((chips, 2 * rows, 2 * rows), F32),
                vmem((2, width, dim), BF16),
                vmem((dim, 2 * rows), F32),
                vmem((dim, 2 * rows), F32),
                vmem((dim, 2 * rows), BF16),
                vmem((dim, 2 * rows), BF16),
                vmem((2 * rows, dim), BF16),
                vmem((2, cols, dim), F32),
                dma((4, 2, arrivals)),
                dma((4, 2, arrivals)),
                dma((4, 2 + 2 * arrivals)),
                dma((4, 2 + 2 * arrivals)),
                dma((n,)),
                dma((n,)),
                dma((chips,)),
                dma((chips,)),
                dma((2, hops, 2)),
                dma((2, hops, 2)),
                dma((6 + width // (2 * rows),)),
            ],
            compiler_params=pltpu.CompilerParams(
                collective_id=0, has_side_effects=True, vmem_limit_bytes=67043328
            ),
        )(
            x_loc,
            dy_loc,
            wq_loc.reshape(width, dim),
            w_key,
            w_value,
            wo_loc.reshape(dim, width),
        )
        results = outs[:5]
        any_spec = [pl.BlockSpec(memory_space=pl.ANY)] * 5
        dx, dwq, dwk, dwv, dwo = pl.pallas_call(
            hand_on,
            name="hand_on",
            out_shape=tuple(sds(o.shape, o.dtype) for o in results),
            in_specs=any_spec,
            out_specs=any_spec,
            scratch_shapes=[vmem(o.shape, o.dtype) for o in results] + [dma((64,)), dma((64,))],
        )(*results)
        return dx, dwq.reshape(width, 1, dim), dwk, dwv, dwo.reshape(1, dim, width)

    return jax.shard_map(
        local_step,
        mesh=mesh,
        in_specs=(tok_spec, tok_spec, P(None, "model", None), P(None, None), P(None, None), P("model", None, None)),
        out_specs=(tok_spec, P("data", "model", None), tok_spec, tok_spec, P(("data", "model"), None, None)),
        check_vma=False,
    )
```

time: 319 us -> 282 us (0.88)
  Pallas kernels: 308 us -> 281 us
  local copies, waits for them, and re-layouts: 9.58 us -> 0 us
    pallas_call x1, Pallas kernels: 308 us -> 277 us  [local_step(): pl.pallas_call(make_kernel(n), name='mqa_backward', out_shape=(sds((rows,...]
    unnamed x5 -> x0, local copies, waits for them, and re-layouts: 9.58 us -> none
    pallas_call x0 -> x1, Pallas kernels: none -> 4.21 us  [local_step(): pl.pallas_call(hand_on, name='hand_on', out_shape=tuple((sds(o.shape, o.d...]
where the time goes in v2:
time: 282 us
  Pallas kernels  281 us (100%)
    pallas_call x1, Pallas kernels, local_step(): pl.pallas_call(make_kernel(n), name='mqa_backward', out_shape=(sds((rows,...  277 us

profile of v2, /device:TPU:21, one launch (start us, length us, event | category | flops | bytes accessed | tf_op | source)
XLA Modules:
  0.0 282.1 jit_solution(14886952707184514722)
XLA Ops:
  0.6 277.2 %mqa_backward.1 = (bf16[256,2048]{1,0:T(8,128)(2,1)}, f32[2048,128]{1,0:T(8,128)}, f32[128,128]{1,0:T(8,128)}, f32[128,128]{1,0:T(8,128)}, f32[128,2048]{1,0:T(8,128)}, /*index=5*/bf16[16,2048,128]{2,1,0:T(8,128)(2,1)}) custom-call(bf16[256,2048]{1,0:T(8,128)(2,1)} %x_hbm.1, bf16[256,2048]{1,0:T(8,128)(2,1)} %dy_hbm.1, bf16[2048,128]{1,0:T(8,128)(2,1)} %bitcast.6, ...), custom_call_target="tpu_custom_call" | custom-call | tf_op jit(solution)/shard_map/mqa_backward/pallas_call | solution.py:511
  277.8 4.2 %hand_on.1 = (bf16[256,2048]{1,0:T(8,128)(2,1)}, f32[2048,128]{1,0:T(8,128)}, f32[128,128]{1,0:T(8,128)}, f32[128,128]{1,0:T(8,128)}, f32[128,2048]{1,0:T(8,128)}) custom-call(bf16[256,2048]{1,0:T(8,128)(2,1)} %get-tuple-element.15.refs_0_, f32[2048,128]{1,0:T(8,128)} %get-tuple-element.16.refs_1_, f32[128,128]{1,0:T(8,128)} %get-tuple-element.17.refs_2_, ...), custom_call_target="tpu_custom_call" | custom-call | tf_op jit(solution)/shard_map/hand_on/pallas_call | solution.py:572

commit v3 on v2

--- a/solution.py
+++ b/solution.py
@@ -39,7 +39,7 @@
     def kernel(
         x_hbm, dy_hbm, wq_hbm, wk_hbm, wv_hbm, wo_hbm,
         dx_hbm, dwq_hbm, dwk_hbm, dwv_hbm, dwo_hbm, wq_all,
-        x_all, dy_all, q_all, kv_all, kt_all, vt_all, wqkv, wo,
+        x_all, dy_all, q_all, kv_all, kt_all, vt_all, o_all, lse, wqkv, wo, wot,
         dkv, part, sums, dq_in, dwqt, dwo_acc, st, wq_st,
         ot, dqt, dot_s, qt_s, do_s, dwkv,
         ring_r, ring_s, pair_r, pair_s, dq_r, dq_s, px_r, px_s, rs_r, rs_s, loc,
@@ -47,7 +47,6 @@
         rows, width = x_hbm.shape
         dim = wk_hbm.shape[1]
         cols = width // n
-        tiles = width // rows
         scale = 1.0 / math.sqrt(dim)
         m = lax.axis_index("model")
         c = lax.div(m, 2)
@@ -61,21 +60,23 @@
                 device_id={"model": dev}, device_id_type=MESH,
             )
 
-        bufs = (x_all, dy_all, wq_all)
+        bufs = (x_all, dy_all)
         owns = (x_hbm, dy_hbm, wq_hbm)
 
-        def half(ref, h):
-            size = ref.shape[0] // 2
-            return ref.at[pl.ds(pl.multiple_of(h * size, size), size), :]
+        def half(ref, h, size, base=0):
+            return ref.at[pl.ds(pl.multiple_of(base + h * size, size), size), :]
 
         def chunk_at(r, blk, h):
+            chip = lax.div(blk, 2)
+            base = lax.rem(blk, 2) * rows
             if r == RG:
-                at = pl.ds(pl.multiple_of(lax.rem(blk, 2) * rows, rows), rows)
-                return kv_all.at[h, lax.div(blk, 2), at, :]
-            return half(bufs[r].at[blk], h)
+                return kv_all.at[h, chip, pl.ds(pl.multiple_of(base, rows), rows), :]
+            if r == RW:
+                return half(wq_all.at[blk], h, width // 2)
+            return half(bufs[r].at[chip], h, rows // 2, base)
 
         def own_at(r, h):
-            return chunk_at(r, m, h) if r == RG else half(owns[r], h)
+            return chunk_at(r, m, h) if r == RG else half(owns[r], h, owns[r].shape[0] // 2)
 
         def start_own(r):
             for p in (0, 1):
@@ -135,20 +136,21 @@
         def local(src, dst, i):
             return pltpu.make_async_copy(src, dst, loc.at[i])
 
+        own_rows = pl.ds(pl.multiple_of(k * rows, rows), rows)
         loads = [
-            local(x_hbm, x_all.at[m], 0),
+            local(x_hbm, x_all.at[c, own_rows, :], 0),
             local(wq_hbm, wqkv.at[:, pl.ds(0, dim)], 1),
             local(wk_hbm, wqkv.at[:, pl.ds(dim, dim)], 2),
             local(wv_hbm, wqkv.at[:, pl.ds(2 * dim, dim)], 3),
             local(wo_hbm, wo, 4),
-            local(dy_hbm, dy_all.at[m], 5),
+            local(dy_hbm, dy_all.at[c, own_rows, :], 5),
         ]
         for load in loads:
             load.start()
         barrier = pltpu.get_barrier_semaphore()
-        for i in range(1, n):
-            pl.semaphore_signal(barrier, inc=1, device_id={"model": lax.rem(m + i, n)}, device_id_type=MESH)
-        pl.semaphore_wait(barrier, n - 1)
+        for dev in (*nbr, mate):
+            pl.semaphore_signal(barrier, inc=1, device_id={"model": dev}, device_id_type=MESH)
+        pl.semaphore_wait(barrier, 3)
         start_own(RX)
         dwqt[...] = jnp.zeros_like(dwqt)
         dwo_acc[...] = jnp.zeros_like(dwo_acc)
@@ -161,16 +163,15 @@
         lax.fori_loop(0, n, clear, 0)
         for load in loads:
             load.wait()
+        wot[...] = wo[...].T
 
         def project(ch):
-            for i in (0, 1):
-                at = pl.ds(i * rows, rows)
-                qkv = dot(x_all[2 * ch + i], wqkv[...]).astype(BF16)
-                q_all[ch, at, :] = qkv[:, :dim]
-                kv_all[0, ch, at, :] = qkv[:, dim : 2 * dim]
-                kv_all[1, ch, at, :] = qkv[:, 2 * dim :]
-                kt_all[ch, :, at] = qkv[:, dim : 2 * dim].T
-                vt_all[ch, :, at] = qkv[:, 2 * dim :].T
+            qkv = dot(x_all[ch], wqkv[...]).astype(BF16)
+            q_all[ch] = qkv[:, :dim]
+            kv_all[0, ch] = qkv[:, dim : 2 * dim]
+            kv_all[1, ch] = qkv[:, 2 * dim :]
+            kt_all[ch] = qkv[:, dim : 2 * dim].T
+            vt_all[ch] = qkv[:, 2 * dim :].T
 
         def gathered(u, _):
             @pl.when(u == 1)
@@ -199,10 +200,11 @@
         factor = scale * math.log2(math.e)
         halves = [pl.ds(i * rows, rows) for i in (0, 1)]
 
-        def attend(ch):
-            for i in (0, 1):
-                do_s[halves[i], :] = dot_nt(dy_all[2 * ch + i], wo[...]).astype(BF16)
-            dot_s[...] = do_s[...].T
+        def causal(i):
+            key = lax.broadcasted_iota(jnp.int32, (rows, pair), 0) + i * rows
+            return key <= lax.broadcasted_iota(jnp.int32, (rows, pair), 1)
+
+        def forward(ch):
             qt_s[...] = q_all[ch].T
 
             def scores(j, top):
@@ -215,9 +217,7 @@
             top = lax.fori_loop(0, ch, scores, jnp.full((8, pair), -jnp.inf, F32))
             for i in (0, 1):
                 s = dot(kv_all[0, ch, halves[i], :], qt_s[...])
-                key = lax.broadcasted_iota(jnp.int32, (rows, pair), 0) + i * rows
-                query = lax.broadcasted_iota(jnp.int32, (rows, pair), 1)
-                s = jnp.where(key <= query, s, -jnp.inf)
+                s = jnp.where(causal(i), s, -jnp.inf)
                 st[ch, halves[i], :] = s
                 top = jnp.maximum(top, rowfold(s, "max"))
             top = jnp.max(top, axis=0, keepdims=True)
@@ -230,33 +230,58 @@
                 return total
 
             total = lax.fori_loop(0, ch + 1, weights, jnp.zeros((8, pair), F32))
-            inv = 1.0 / jnp.sum(total, axis=0, keepdims=True)
+            total = jnp.sum(total, axis=0, keepdims=True)
+            lse[ch] = jnp.broadcast_to(top * factor + jnp.log2(total), (8, pair))
+            inv = 1.0 / total
             ot[...] = jnp.zeros_like(ot)
+
+            def outputs(j, _):
+                ot[...] += dot(vt_all[j], (st[j] * inv).astype(BF16))
+                return 0
+
+            lax.fori_loop(0, ch + 1, outputs, 0)
+            o_all[ch] = ot[...].astype(BF16)
+
+        def forwarded(u, _):
+            @pl.when(u == hops)
+            def _():
+                service(RW, 1)
+
+            forward(chip_at(u))
+            return 0
+
+        service(RW, 0)
+        lax.fori_loop(0, chips, forwarded, 0)
+
+        def attend(ch):
+            do_s[...] = dot(dy_all[ch], wot[...]).astype(BF16)
+            dot_s[...] = do_s[...].T
+            qt_s[...] = q_all[ch].T
+            row = jnp.sum(dot_s[...].astype(F32) * o_all[ch].astype(F32), axis=0, keepdims=True)
+            shift = lse[ch, 0:1, :]
             dqt[...] = jnp.zeros_like(dqt)
 
-            def outputs(j, _):
-                p = (st[j] * inv).astype(BF16)
-                ot[...] += dot(vt_all[j], p)
-                dv = dot(p, do_s[...])
+            def tile(j, masked):
+                add_q = 0.0
                 for i in (0, 1):
-                    dkv[2 * j + i, 1] += dv[i * rows : (i + 1) * rows]
+                    at = halves[i]
+                    s = dot(kv_all[0, j, at, :], qt_s[...])
+                    p = jnp.exp2(s * factor - shift)
+                    if masked:
+                        p = jnp.where(causal(i), p, 0.0)
+                    dp = dot(kv_all[1, j, at, :], dot_s[...])
+                    g = (p * (dp - row) * scale).astype(BF16)
+                    dkv[2 * j + i, 1] += dot(p.astype(BF16), do_s[...])
+                    dkv[2 * j + i, 0] += dot(g, q_all[ch])
+                    add_q += dot(kt_all[j, :, at], g)
+                dqt[...] += add_q
+
+            def grads(j, _):
+                tile(j, False)
                 return 0
 
-            lax.fori_loop(0, ch + 1, outputs, 0)
-            o = ot[...].astype(BF16)
-            row = jnp.sum(dot_s[...].astype(F32) * o.astype(F32), axis=0, keepdims=True)
-            inv_scale = inv * scale
-
-            def grads(j, _):
-                dp = dot(kv_all[1, j], dot_s[...])
-                g = ((st[j] * inv_scale) * (dp - row)).astype(BF16)
-                dqt[...] += dot(kt_all[j], g)
-                dk = dot(g, q_all[ch])
-                for i in (0, 1):
-                    dkv[2 * j + i, 0] += dk[i * rows : (i + 1) * rows]
-                return 0
-
-            lax.fori_loop(0, ch + 1, grads, 0)
+            lax.fori_loop(0, ch, grads, 0)
+            tile(ch, True)
             dq = dqt[...].astype(BF16)
             q_all[ch] = dq.T
             for i in (0, 1):
@@ -266,21 +291,19 @@
                 def _():
                     remote(q_all.at[ch, halves[i], :], dq_in.at[m], dq_s.at[blk], dq_r.at[m], blk).start()
 
-            for t in range(tiles):
-                at = pl.ds(t * rows, rows)
-                add_q = dot(dq[:, :rows], x_all[2 * ch, :, at])
-                add_o = dot(o[:, :rows], dy_all[2 * ch, :, at])
-                dwqt[:, at] += add_q + dot(dq[:, rows:], x_all[2 * ch + 1, :, at])
-                dwo_acc[:, at] += add_o + dot(o[:, rows:], dy_all[2 * ch + 1, :, at])
+            for t in range(width // pair):
+                at = pl.ds(t * pair, pair)
+                dwqt[:, at] += dot(dq, x_all[ch, :, at])
+                dwo_acc[:, at] += dot(o_all[ch], dy_all[ch, :, at])
 
         def attended(u, _):
             @pl.when(u == 1)
             def _():
-                for a in range(1, last - 3):
+                for a in range(2, last - 3):
                     service(RW, a)
                 service(RY, 0)
 
-            @pl.when((u >= 1) & (u <= last))
+            @pl.when((u >= 1) & (u < last))
             def _():
                 service(RY, u)
 
@@ -288,12 +311,15 @@
             def _():
                 service(RW, last - 3)
                 service(RW, last - 2)
+
+            @pl.when(u == chips - 1)
+            def _():
+                service(RY, last)
 
             wait_pair(RY, u)
             attend(chip_at(u))
             return 0
 
-        service(RW, 0)
         lax.fori_loop(0, chips, attended, 0)
 
         order = [hops]
@@ -384,7 +410,7 @@
 
         gather(0)
         hop(1)
-        add_dx(q_all[c, pl.ds(pl.multiple_of(k * rows, rows), rows), :], wqkv.at[:, pl.ds(0, dim)])
+        add_dx(q_all[c, own_rows, :], wqkv.at[:, pl.ds(0, dim)])
         dx_heads(1, 3)
         gather(1)
         gather(2)
@@ -400,9 +426,8 @@
             done += 4
 
         def turn(j, _):
-            for i in (0, 1):
-                xs = x_all[2 * j + i, :, pl.ds(pl.multiple_of(m * cols, cols), cols)]
-                kt_all[j, pl.ds(0, cols), halves[i]] = xs.T
+            xs = x_all[j, :, pl.ds(pl.multiple_of(m * cols, cols), cols)]
+            kt_all[j, pl.ds(0, cols), :] = xs.T
             return 0
 
         lax.fori_loop(0, chips, turn, 0)
@@ -424,8 +449,8 @@
         dx_head(n - 1)
         wait_sends(RY)
         for t in range(spare):
-            dy_all[0, :, pl.ds(t * pair, pair)] = st[t, pl.ds(0, rows), :].astype(BF16)
-        dx_out = local(dy_all.at[0], dx_hbm, 4)
+            dy_all[0, pl.ds(0, rows), pl.ds(t * pair, pair)] = st[t, pl.ds(0, rows), :].astype(BF16)
+        dx_out = local(dy_all.at[0, pl.ds(0, rows), :], dx_hbm, 4)
         dx_out.start()
 
         def last_steps(u, _):
@@ -522,14 +547,17 @@
             in_specs=[pl.BlockSpec(memory_space=pl.ANY)] * 6,
             out_specs=[pl.BlockSpec(memory_space=pl.ANY)] * 6,
             scratch_shapes=[
-                vmem((n, rows, width), BF16),
-                vmem((n, rows, width), BF16),
+                vmem((chips, 2 * rows, width), BF16),
+                vmem((chips, 2 * rows, width), BF16),
                 vmem((chips, 2 * rows, dim), BF16),
                 vmem((2, chips, 2 * rows, dim), BF16),
                 vmem((chips, dim, 2 * rows), BF16),
                 vmem((chips, dim, 2 * rows), BF16),
+                vmem((chips, dim, 2 * rows), BF16),
+                vmem((chips, 8, 2 * rows), F32),
                 vmem((width, 3 * dim), BF16),
                 vmem((dim, width), BF16),
+                vmem((width, dim), BF16),
                 vmem((n, 2, rows, dim), F32),
                 vmem((chips, 2, rows, dim), F32),
                 vmem((2, hops, 2, rows, dim), F32),

time: 282 us -> 278 us (0.986)
  Pallas kernels: 281 us -> 277 us
    pallas_call x1, Pallas kernels: 277 us -> 273 us  [local_step(): pl.pallas_call(make_kernel(n), name='mqa_backward', out_shape=(sds((rows,...]
where the time goes in v3:
time: 278 us
  Pallas kernels  277 us (100%)
    pallas_call x1, Pallas kernels, local_step(): pl.pallas_call(make_kernel(n), name='mqa_backward', out_shape=(sds((rows,...  273 us

profile of v3, /device:TPU:21, one launch (start us, length us, event | category | flops | bytes accessed | tf_op | source)
XLA Modules:
  0.0 277.9 jit_solution(14924078570079689598)
XLA Ops:
  0.6 273.0 %mqa_backward.1 = (bf16[256,2048]{1,0:T(8,128)(2,1)}, f32[2048,128]{1,0:T(8,128)}, f32[128,128]{1,0:T(8,128)}, f32[128,128]{1,0:T(8,128)}, f32[128,2048]{1,0:T(8,128)}, /*index=5*/bf16[16,2048,128]{2,1,0:T(8,128)(2,1)}) custom-call(bf16[256,2048]{1,0:T(8,128)(2,1)} %x_hbm.1, bf16[256,2048]{1,0:T(8,128)(2,1)} %dy_hbm.1, bf16[2048,128]{1,0:T(8,128)(2,1)} %bitcast.6, ...), custom_call_target="tpu_custom_call" | custom-call | tf_op jit(solution)/shard_map/mqa_backward/pallas_call | solution.py:536
  273.7 4.2 %hand_on.1 = (bf16[256,2048]{1,0:T(8,128)(2,1)}, f32[2048,128]{1,0:T(8,128)}, f32[128,128]{1,0:T(8,128)}, f32[128,128]{1,0:T(8,128)}, f32[128,2048]{1,0:T(8,128)}) custom-call(bf16[256,2048]{1,0:T(8,128)(2,1)} %get-tuple-element.15.refs_0_, f32[2048,128]{1,0:T(8,128)} %get-tuple-element.16.refs_1_, f32[128,128]{1,0:T(8,128)} %get-tuple-element.17.refs_2_, ...), custom_call_target="tpu_custom_call" | custom-call | tf_op jit(solution)/shard_map/hand_on/pallas_call | solution.py:600

commit v4 on v3

--- a/solution.py
+++ b/solution.py
@@ -10,7 +10,7 @@
 BF16 = jnp.bfloat16
 F32 = jnp.float32
 MESH = pl.DeviceIdType.MESH
-RX, RY, RW, RG = range(4)
+RX, RY, RW = range(3)
 
 
 def dot(a, b):
@@ -41,12 +41,15 @@
         dx_hbm, dwq_hbm, dwk_hbm, dwv_hbm, dwo_hbm, wq_all,
         x_all, dy_all, q_all, kv_all, kt_all, vt_all, o_all, lse, wqkv, wo, wot,
         dkv, part, sums, dq_in, dwqt, dwo_acc, st, wq_st,
-        ot, dqt, dot_s, qt_s, do_s, dwkv,
-        ring_r, ring_s, pair_r, pair_s, dq_r, dq_s, px_r, px_s, rs_r, rs_s, loc,
+        ot, dqt, dot_s, qt_s, thin, kv_rows, dw_out, dw_in, dw_t,
+        ring_r, ring_s, pair_r, pair_s, dq_r, dq_s, px_r, px_s, rs_r, rs_s,
+        kv_r, kv_s, dw_r, dw_s, loc,
     ):
         rows, width = x_hbm.shape
         dim = wk_hbm.shape[1]
         cols = width // n
+        slim = 2 * dim // n
+        quarter = chips // 2
         scale = 1.0 / math.sqrt(dim)
         m = lax.axis_index("model")
         c = lax.div(m, 2)
@@ -69,14 +72,12 @@
         def chunk_at(r, blk, h):
             chip = lax.div(blk, 2)
             base = lax.rem(blk, 2) * rows
-            if r == RG:
-                return kv_all.at[h, chip, pl.ds(pl.multiple_of(base, rows), rows), :]
             if r == RW:
                 return half(wq_all.at[blk], h, width // 2)
             return half(bufs[r].at[chip], h, rows // 2, base)
 
         def own_at(r, h):
-            return chunk_at(r, m, h) if r == RG else half(owns[r], h, owns[r].shape[0] // 2)
+            return half(owns[r], h, owns[r].shape[0] // 2)
 
         def start_own(r):
             for p in (0, 1):
@@ -154,13 +155,14 @@
         start_own(RX)
         dwqt[...] = jnp.zeros_like(dwqt)
         dwo_acc[...] = jnp.zeros_like(dwo_acc)
-        dwkv[...] = jnp.zeros_like(dwkv)
 
         def clear(j, _):
-            dkv[j] = jnp.zeros(dkv.shape[1:], F32)
+            for kind in (0, 1):
+                for hi in (0, 1):
+                    dkv[kind, hi, j] = jnp.zeros(dkv.shape[3:], F32)
             return 0
 
-        lax.fori_loop(0, n, clear, 0)
+        lax.fori_loop(0, quarter, clear, 0)
         for load in loads:
             load.wait()
         wot[...] = wo[...].T
@@ -254,8 +256,7 @@
         lax.fori_loop(0, chips, forwarded, 0)
 
         def attend(ch):
-            do_s[...] = dot(dy_all[ch], wot[...]).astype(BF16)
-            dot_s[...] = do_s[...].T
+            dot_s[...] = dot(dy_all[ch], wot[...]).astype(BF16).T
             qt_s[...] = q_all[ch].T
             row = jnp.sum(dot_s[...].astype(F32) * o_all[ch].astype(F32), axis=0, keepdims=True)
             shift = lse[ch, 0:1, :]
@@ -263,6 +264,7 @@
 
             def tile(j, masked):
                 add_q = 0.0
+                hi, lo = lax.div(j, quarter), lax.rem(j, quarter)
                 for i in (0, 1):
                     at = halves[i]
                     s = dot(kv_all[0, j, at, :], qt_s[...])
@@ -271,8 +273,8 @@
                         p = jnp.where(causal(i), p, 0.0)
                     dp = dot(kv_all[1, j, at, :], dot_s[...])
                     g = (p * (dp - row) * scale).astype(BF16)
-                    dkv[2 * j + i, 1] += dot(p.astype(BF16), do_s[...])
-                    dkv[2 * j + i, 0] += dot(g, q_all[ch])
+                    dkv[1, hi, lo, :, at] += dot_nt(dot_s[...], p.astype(BF16))
+                    dkv[0, hi, lo, :, at] += dot_nt(qt_s[...], g)
                     add_q += dot(kt_all[j, :, at], g)
                 dqt[...] += add_q
 
@@ -284,22 +286,25 @@
             tile(ch, True)
             dq = dqt[...].astype(BF16)
             q_all[ch] = dq.T
-            for i in (0, 1):
-                blk = 2 * ch + i
-
-                @pl.when(blk != m)
-                def _():
-                    remote(q_all.at[ch, halves[i], :], dq_in.at[m], dq_s.at[blk], dq_r.at[m], blk).start()
-
             for t in range(width // pair):
                 at = pl.ds(t * pair, pair)
                 dwqt[:, at] += dot(dq, x_all[ch, :, at])
                 dwo_acc[:, at] += dot(o_all[ch], dy_all[ch, :, at])
 
+        def send_dq(u, i):
+            ch = chip_at(u)
+            blk = 2 * ch + i
+
+            @pl.when(blk != m)
+            def _():
+                remote(q_all.at[ch, halves[i], :], dq_in.at[m], dq_s.at[blk], dq_r.at[m], blk).start()
+
+        late = chips - 1
+
         def attended(u, _):
             @pl.when(u == 1)
             def _():
-                for a in range(2, last - 3):
+                for a in range(2, last - 1 - 2):
                     service(RW, a)
                 service(RY, 0)
 
@@ -309,8 +314,8 @@
 
             @pl.when(u == last - 2)
             def _():
-                service(RW, last - 3)
-                service(RW, last - 2)
+                service(RW, last - 2 - 1)
+                service(RW, last - 2 - 0)
 
             @pl.when(u == chips - 1)
             def _():
@@ -318,6 +323,12 @@
 
             wait_pair(RY, u)
             attend(chip_at(u))
+
+            @pl.when(u < late)
+            def _():
+                send_dq(u, 0)
+                send_dq(u, 1)
+
             return 0
 
         lax.fori_loop(0, chips, attended, 0)
@@ -330,9 +341,13 @@
         def chip_off(off):
             return lax.rem(c + off + chips, chips)
 
+        def slice_of(dev):
+            row = pl.multiple_of(lax.rem(dev, chips) * slim, slim)
+            return dkv.at[lax.div(dev, chips), :, :, pl.ds(row, slim), :]
+
         def px(i):
             chip = chip_off(order[i])
-            return remote(dkv.at[2 * chip + 1 - k], part.at[chip], px_s.at[i], px_r.at[i], mate)
+            return remote(slice_of(2 * chip + 1 - k), part.at[chip], px_s.at[i], px_r.at[i], mate)
 
         for i in range(chips):
             px(i).start()
@@ -385,7 +400,7 @@
         def gather(i):
             px(i).wait_recv()
             chip = chip_off(order[i])
-            part[chip] += dkv[2 * chip + k]
+            part[chip] += slice_of(2 * chip + k)[...]
 
         def rs(d, t, h, src):
             return remote(src, sums.at[d, t - 1, h], rs_s.at[d, t - 1, h], rs_r.at[d, t - 1, h], nbr[d])
@@ -393,12 +408,13 @@
         sent = []
 
         def hop(t):
-            for d in (0, 1):
-                chip = chip_off((hops + 1 - t) * (1 - 2 * d))
-                for h in (d, 1 - d):
-                    if t == 1 and h != d:
+            for first in (True, False):
+                for d in (0, 1):
+                    h = d if first else 1 - d
+                    chip = chip_off((hops + 1 - t) * (1 - 2 * d))
+                    if t == 1 and not first:
                         continue
-                    if t == 1 or (t == 2 and h != d):
+                    if t == 1 or (t == 2 and not first):
                         copy = rs(d, t, h, part.at[chip, h])
                     else:
                         held = sums.at[d, t - 2, h]
@@ -415,71 +431,97 @@
         gather(1)
         gather(2)
         hop(2)
-        dx_heads(3, 5)
         for i in range(3, chips):
             gather(i)
+        dx_heads(3, 5)
         done = 5
         for t in range(3, hops + 1):
             hop(t)
             service(RW, last - hops + t)
-            dx_heads(done, done + 4)
-            done += 4
-
-        def turn(j, _):
-            xs = x_all[j, :, pl.ds(pl.multiple_of(m * cols, cols), cols)]
-            kt_all[j, pl.ds(0, cols), :] = xs.T
-            return 0
-
-        lax.fori_loop(0, chips, turn, 0)
+            send_dq(chips - 1, t - hops + 1)
+            dx_heads(done, done + 2)
+            done += 2
+
         for h in (0, 1):
             total = part[c, h]
             for d in (0, 1):
                 held = sums.at[d, hops - 1, h]
                 rs(d, hops, h, held).wait_recv()
                 total += held[...]
-            chunk_at(RG, m, h)[...] = total.astype(BF16)
-        start_own(RG)
-        own_kv = [chunk_at(RG, m, h)[...] for h in (0, 1)]
+            thin[h] = total.astype(BF16)
+
+        def tokens_of(dev):
+            chip = lax.div(dev, 2)
+            at = pl.ds(pl.multiple_of(lax.rem(dev, 2) * rows, rows), rows)
+            return thin.at[lax.div(chip, quarter), lax.rem(chip, quarter), :, at]
+
+        def kv_copy(i):
+            dev = lax.rem(m + i, n)
+            return remote(tokens_of(dev), kv_rows.at[m], kv_s.at[i], kv_r.at[i], dev)
+
+        far = sorted(range(1, n), key=lambda i: -min(i, n - i))
+        for i in far:
+            kv_copy(i).start()
+        kv_rows[m] = tokens_of(m)[...]
+
+        def dw_copy(dev):
+            return remote(dw_out.at[dev], dw_in.at[m], dw_s.at[dev], dw_r.at[m], dev)
+
+        per = pair // cols
+
+        def key_grads(t, _):
+            at = pl.ds(pl.multiple_of(t * pair, pair), pair)
+            add = dot(thin[0, 0], x_all[0, :, at])
+            for j in range(1, chips):
+                add += dot(thin[j // quarter, j % quarter], x_all[j, :, at])
+            for i in range(per):
+                dw_out[t * per + i] = add[:, i * cols : (i + 1) * cols]
+            for i in range(per):
+                dev = t * per + i
+
+                @pl.when(dev != m)
+                def _():
+                    dw_copy(dev).start()
+
+            return 0
+
+        lax.fori_loop(0, width // pair, key_grads, 0)
+        dx_heads(done, n)
+        dx_head(n - 1)
+        for i in far:
+            kv_copy(i).wait_recv()
+        own_kv = kv_rows[...].reshape(2 * dim, rows).T
+        wait_sends(RY)
         for t in range(spare):
             at = pl.ds(t * pair, pair)
-            add = dot_nt(own_kv[0], wqkv[at, pl.ds(dim, dim)])
-            add += dot_nt(own_kv[1], wqkv[at, pl.ds(2 * dim, dim)])
-            st[t, pl.ds(0, rows), :] += add
-        dx_heads(done, n)
-        dx_head(n - 1)
-        wait_sends(RY)
-        for t in range(spare):
-            dy_all[0, pl.ds(0, rows), pl.ds(t * pair, pair)] = st[t, pl.ds(0, rows), :].astype(BF16)
+            add = dot_nt(own_kv, wqkv[at, pl.ds(dim, 2 * dim)])
+            dy_all[0, pl.ds(0, rows), at] = (st[t, pl.ds(0, rows), :] + add).astype(BF16)
         dx_out = local(dy_all.at[0, pl.ds(0, rows), :], dx_hbm, 4)
         dx_out.start()
-
-        def last_steps(u, _):
-            @pl.when(u == 1)
-            def _():
-                service(RG, 0)
-
-            @pl.when((u >= 1) & (u <= last))
-            def _():
-                service(RG, u)
-
-            wait_pair(RG, u)
-            ch = chip_at(u)
-            for h in (0, 1):
-                dwkv[h] += dot(kt_all[ch, pl.ds(0, cols), :], kv_all[h, ch])
+        dw_in[m] = dw_out[m]
+
+        def arrived(dev, _):
+            @pl.when(dev != m)
+            def _():
+                dw_copy(dev).wait_send()
+                remote(dw_in.at[dev], dw_in.at[dev], dw_s.at[dev], dw_r.at[dev], mate).wait_recv()
+
             return 0
 
-        lax.fori_loop(0, chips, last_steps, 0)
-        outs = [
-            local(dwkv.at[0], dwk_hbm, 2),
-            local(dwkv.at[1], dwv_hbm, 3),
-        ]
+        lax.fori_loop(0, n, arrived, 0)
+        turned = dw_in[...].reshape(2 * dim, cols)
+        dw_t[0] = turned[:dim].T
+        dw_t[1] = turned[dim:].T
+        outs = [local(dw_t.at[0], dwk_hbm, 2), local(dw_t.at[1], dwv_hbm, 3)]
         for out in outs:
             out.start()
         for out in (dwo_out, *dwq_out, dx_out, *outs):
             out.wait()
 
-        for r in (RX, RW, RG):
+        for r in (RX, RW):
             wait_sends(r)
+        for i in far:
+            kv_copy(i).wait_send()
         for i in range(chips):
             px(i).wait_send()
         for copy in sent:
@@ -533,6 +575,7 @@
         vmem = pltpu.VMEM
         dma = pltpu.SemaphoreType.DMA
         arrivals = 2 * hops - 1
+        slim = 2 * dim // n
         outs = pl.pallas_call(
             make_kernel(n),
             name="mqa_backward",
@@ -558,9 +601,9 @@
                 vmem((width, 3 * dim), BF16),
                 vmem((dim, width), BF16),
                 vmem((width, dim), BF16),
-                vmem((n, 2, rows, dim), F32),
-                vmem((chips, 2, rows, dim), F32),
-                vmem((2, hops, 2, rows, dim), F32),
+                vmem((2, 2, hops, dim, 2 * rows), F32),
+                vmem((chips, 2, hops, slim, 2 * rows), F32),
+                vmem((2, hops, 2, hops, slim, 2 * rows), F32),
                 vmem((n, rows, dim), BF16),
                 vmem((dim, width), F32),
                 vmem((dim, width), F32),
@@ -570,18 +613,25 @@
                 vmem((dim, 2 * rows), F32),
                 vmem((dim, 2 * rows), BF16),
                 vmem((dim, 2 * rows), BF16),
-                vmem((2 * rows, dim), BF16),
+                vmem((2, hops, slim, 2 * rows), BF16),
+                vmem((n, slim, rows), BF16),
+                vmem((n, slim, cols), F32),
+                vmem((n, slim, cols), F32),
                 vmem((2, cols, dim), F32),
-                dma((4, 2, arrivals)),
-                dma((4, 2, arrivals)),
-                dma((4, 2 + 2 * arrivals)),
-                dma((4, 2 + 2 * arrivals)),
+                dma((3, 2, arrivals)),
+                dma((3, 2, arrivals)),
+                dma((3, 2 + 2 * arrivals)),
+                dma((3, 2 + 2 * arrivals)),
                 dma((n,)),
                 dma((n,)),
                 dma((chips,)),
                 dma((chips,)),
                 dma((2, hops, 2)),
                 dma((2, hops, 2)),
+                dma((n,)),
+                dma((n,)),
+                dma((n,)),
+                dma((n,)),
                 dma((6 + width // (2 * rows),)),
             ],
             compiler_params=pltpu.CompilerParams(

time: 278 us -> 269 us (0.968)
  Pallas kernels: 277 us -> 265 us
    pallas_call x1, Pallas kernels: 273 us -> 261 us  [local_step(): pl.pallas_call(make_kernel(n), name='mqa_backward', out_shape=(sds((rows,...]
where the time goes in v4:
time: 269 us; the launch traced here: 266 us
  Pallas kernels  265 us (99%)
    pallas_call x1, Pallas kernels, local_step(): pl.pallas_call(make_kernel(n), name='mqa_backward', out_shape=(sds((rows,...  261 us

profile of v4, /device:TPU:21, one launch (start us, length us, event | category | flops | bytes accessed | tf_op | source)
XLA Modules:
  0.0 266.2 jit_solution(12420190902194398179)
XLA Ops:
  0.6 261.2 %mqa_backward.1 = (bf16[256,2048]{1,0:T(8,128)(2,1)}, f32[2048,128]{1,0:T(8,128)}, f32[128,128]{1,0:T(8,128)}, f32[128,128]{1,0:T(8,128)}, f32[128,2048]{1,0:T(8,128)}, /*index=5*/bf16[16,2048,128]{2,1,0:T(8,128)(2,1)}) custom-call(bf16[256,2048]{1,0:T(8,128)(2,1)} %x_hbm.1, bf16[256,2048]{1,0:T(8,128)(2,1)} %dy_hbm.1, bf16[2048,128]{1,0:T(8,128)(2,1)} %bitcast.6, ...), custom_call_target="tpu_custom_call" | custom-call | tf_op jit(solution)/shard_map/mqa_backward/pallas_call | solution.py:579
  261.8 4.2 %hand_on.1 = (bf16[256,2048]{1,0:T(8,128)(2,1)}, f32[2048,128]{1,0:T(8,128)}, f32[128,128]{1,0:T(8,128)}, f32[128,128]{1,0:T(8,128)}, f32[128,2048]{1,0:T(8,128)}) custom-call(bf16[256,2048]{1,0:T(8,128)(2,1)} %get-tuple-element.15.refs_0_, f32[2048,128]{1,0:T(8,128)} %get-tuple-element.16.refs_1_, f32[128,128]{1,0:T(8,128)} %get-tuple-element.17.refs_2_, ...), custom_call_target="tpu_custom_call" | custom-call | tf_op jit(solution)/shard_map/hand_on/pallas_call | solution.py:650

commit v5 on v4

--- a/solution.py
+++ b/solution.py
@@ -426,21 +426,17 @@
 
         gather(0)
         hop(1)
+        service(RW, last - 1)
         add_dx(q_all[c, own_rows, :], wqkv.at[:, pl.ds(0, dim)])
-        dx_heads(1, 3)
-        gather(1)
-        gather(2)
+        dx_heads(1, late + 3)
+        service(RW, last)
+        for i in range(1, chips):
+            gather(i)
         hop(2)
-        for i in range(3, chips):
-            gather(i)
-        dx_heads(3, 5)
-        done = 5
-        for t in range(3, hops + 1):
+        for t in range(3, hops):
             hop(t)
-            service(RW, last - hops + t)
-            send_dq(chips - 1, t - hops + 1)
-            dx_heads(done, done + 2)
-            done += 2
+        dx_heads(late + 3, n - 2)
+        hop(hops)
 
         for h in (0, 1):
             total = part[c, h]
@@ -462,6 +458,8 @@
         far = sorted(range(1, n), key=lambda i: -min(i, n - i))
         for i in far:
             kv_copy(i).start()
+        send_dq(chips - 1, 0)
+        send_dq(chips - 1, 1)
         kv_rows[m] = tokens_of(m)[...]
 
         def dw_copy(dev):
@@ -486,7 +484,7 @@
             return 0
 
         lax.fori_loop(0, width // pair, key_grads, 0)
-        dx_heads(done, n)
+        dx_heads(n - 2, n)
         dx_head(n - 1)
         for i in far:
             kv_copy(i).wait_recv()

time: 269 us -> 267 us (level)
  no operation moved by 1% of the time
where the time goes in v5:
time: 267 us; the launch traced here: 266 us
  Pallas kernels  265 us (99%)
    pallas_call x1, Pallas kernels, local_step(): pl.pallas_call(make_kernel(n), name='mqa_backward', out_shape=(sds((rows,...  261 us

profile of v5, /device:TPU:21, one launch (start us, length us, event | category | flops | bytes accessed | tf_op | source)
XLA Modules:
  0.0 266.1 jit_solution(180473829223772835)
XLA Ops:
  0.6 261.1 %mqa_backward.1 = (bf16[256,2048]{1,0:T(8,128)(2,1)}, f32[2048,128]{1,0:T(8,128)}, f32[128,128]{1,0:T(8,128)}, f32[128,128]{1,0:T(8,128)}, f32[128,2048]{1,0:T(8,128)}, /*index=5*/bf16[16,2048,128]{2,1,0:T(8,128)(2,1)}) custom-call(bf16[256,2048]{1,0:T(8,128)(2,1)} %x_hbm.1, bf16[256,2048]{1,0:T(8,128)(2,1)} %dy_hbm.1, bf16[2048,128]{1,0:T(8,128)(2,1)} %bitcast.6, ...), custom_call_target="tpu_custom_call" | custom-call | tf_op jit(solution)/shard_map/mqa_backward/pallas_call | solution.py:577
  261.7 4.2 %hand_on.1 = (bf16[256,2048]{1,0:T(8,128)(2,1)}, f32[2048,128]{1,0:T(8,128)}, f32[128,128]{1,0:T(8,128)}, f32[128,128]{1,0:T(8,128)}, f32[128,2048]{1,0:T(8,128)}) custom-call(bf16[256,2048]{1,0:T(8,128)(2,1)} %get-tuple-element.15.refs_0_, f32[2048,128]{1,0:T(8,128)} %get-tuple-element.16.refs_1_, f32[128,128]{1,0:T(8,128)} %get-tuple-element.17.refs_2_, ...), custom_call_target="tpu_custom_call" | custom-call | tf_op jit(solution)/shard_map/hand_on/pallas_call | solution.py:648

commit v6 on v5

--- a/solution.py
+++ b/solution.py
@@ -30,7 +30,7 @@
     return jnp.max(y, axis=0) if op == "max" else jnp.sum(y, axis=0)
 
 
-def make_kernel(n):
+def make_kernel(n, groups):
     chips = n // 2
     hops = chips // 2
     last = 2 * (hops - 1)
@@ -39,11 +39,11 @@
     def kernel(
         x_hbm, dy_hbm, wq_hbm, wk_hbm, wv_hbm, wo_hbm,
         dx_hbm, dwq_hbm, dwk_hbm, dwv_hbm, dwo_hbm, wq_all,
-        x_all, dy_all, q_all, kv_all, kt_all, vt_all, o_all, lse, wqkv, wo, wot,
+        x_all, dy_all, q_all, kv_all, kt_all, vo_all, lse, wqkv, wot,
         dkv, part, sums, dq_in, dwqt, dwo_acc, st, wq_st,
-        ot, dqt, dot_s, qt_s, thin, kv_rows, dw_out, dw_in, dw_t,
+        dqt, dot_s, qt_s, thin, kv_rows, dw_out, dw_in, dw_t,
         ring_r, ring_s, pair_r, pair_s, dq_r, dq_s, px_r, px_s, rs_r, rs_s,
-        kv_r, kv_s, dw_r, dw_s, loc,
+        kv_r, kv_s, dw_r, dw_s, peer_r, peer_s, loc,
     ):
         rows, width = x_hbm.shape
         dim = wk_hbm.shape[1]
@@ -52,6 +52,8 @@
         quarter = chips // 2
         scale = 1.0 / math.sqrt(dim)
         m = lax.axis_index("model")
+        g = lax.axis_index("data")
+        share = width // groups
         c = lax.div(m, 2)
         k = lax.rem(m, 2)
         mate = m + 1 - 2 * k
@@ -73,10 +75,12 @@
             chip = lax.div(blk, 2)
             base = lax.rem(blk, 2) * rows
             if r == RW:
-                return half(wq_all.at[blk], h, width // 2)
+                return half(wq_all.at[blk], h, share // 2, g * share)
             return half(bufs[r].at[chip], h, rows // 2, base)
 
         def own_at(r, h):
+            if r == RW:
+                return half(wq_hbm, h, share // 2, g * share)
             return half(owns[r], h, owns[r].shape[0] // 2)
 
         def start_own(r):
@@ -143,15 +147,20 @@
             local(wq_hbm, wqkv.at[:, pl.ds(0, dim)], 1),
             local(wk_hbm, wqkv.at[:, pl.ds(dim, dim)], 2),
             local(wv_hbm, wqkv.at[:, pl.ds(2 * dim, dim)], 3),
-            local(wo_hbm, wo, 4),
             local(dy_hbm, dy_all.at[c, own_rows, :], 5),
         ]
+        pair = 2 * rows
+        for t in range(width // pair):
+            loads.append(local(wo_hbm.at[:, pl.ds(t * pair, pair)], vo_all.at[t], 6 + t))
         for load in loads:
             load.start()
         barrier = pltpu.get_barrier_semaphore()
         for dev in (*nbr, mate):
             pl.semaphore_signal(barrier, inc=1, device_id={"model": dev}, device_id_type=MESH)
-        pl.semaphore_wait(barrier, 3)
+        for i in range(1, groups):
+            pl.semaphore_signal(barrier, inc=1, device_id={"data": lax.rem(g + i, groups), "model": m}, device_id_type=MESH)
+        pl.semaphore_wait(barrier, 2 + groups)
+        start_own(RW)
         start_own(RX)
         dwqt[...] = jnp.zeros_like(dwqt)
         dwo_acc[...] = jnp.zeros_like(dwo_acc)
@@ -165,7 +174,40 @@
         lax.fori_loop(0, quarter, clear, 0)
         for load in loads:
             load.wait()
-        wot[...] = wo[...].T
+        for t in range(width // pair):
+            wot[pl.ds(t * pair, pair), :] = vo_all[t].T
+
+        def rows_at(group):
+            return wq_all.at[:, pl.ds(pl.multiple_of(group * share, share), share), :]
+
+        def peer(i):
+            there = rows_at(g)
+            return pltpu.make_async_remote_copy(
+                src_ref=there, dst_ref=there, send_sem=peer_s.at[i], recv_sem=peer_r.at[i],
+                device_id={"data": lax.rem(g + i, groups), "model": m}, device_id_type=MESH,
+            )
+
+        mine = pl.ds(pl.multiple_of(g * share, share), share)
+        own_rows_out = local(wqkv.at[mine, pl.ds(0, dim)], wq_all.at[m, mine, :], 1)
+        own_rows_out.start()
+
+        def spread():
+            def waited(u, _):
+                wait_pair(RW, u)
+                return 0
+
+            lax.fori_loop(0, chips, waited, 0)
+            own_rows_out.wait()
+            for i in range(1, groups):
+                peer(i).start()
+
+        def gathered_weights():
+            for i in range(1, groups):
+                there = rows_at(lax.rem(g + groups - i, groups))
+                pltpu.make_async_remote_copy(
+                    src_ref=there, dst_ref=there, send_sem=peer_s.at[i], recv_sem=peer_r.at[i],
+                    device_id={"data": lax.rem(g + i, groups), "model": m}, device_id_type=MESH,
+                ).wait_recv()
 
         def project(ch):
             qkv = dot(x_all[ch], wqkv[...]).astype(BF16)
@@ -173,24 +215,33 @@
             kv_all[0, ch] = qkv[:, dim : 2 * dim]
             kv_all[1, ch] = qkv[:, 2 * dim :]
             kt_all[ch] = qkv[:, dim : 2 * dim].T
-            vt_all[ch] = qkv[:, 2 * dim :].T
+            vo_all[ch] = qkv[:, 2 * dim :].T
 
         def gathered(u, _):
             @pl.when(u == 1)
             def _():
                 service(RX, 0)
 
+            @pl.when((u >= 1) & (u < hops))
+            def _():
+                service(RW, 2 * u - 2)
+                service(RW, 2 * u - 1)
+
+            @pl.when(u == hops)
+            def _():
+                service(RW, last)
+
             @pl.when((u >= 1) & (u <= last))
             def _():
                 service(RX, u)
 
             @pl.when(u == last - 2)
             def _():
-                start_own(RW)
-
-            @pl.when(u == last)
-            def _():
                 start_own(RY)
+
+            @pl.when(u == hops + 1)
+            def _():
+                spread()
 
             wait_pair(RX, u)
             project(chip_at(u))
@@ -198,7 +249,6 @@
 
         lax.fori_loop(0, chips, gathered, 0)
 
-        pair = 2 * rows
         factor = scale * math.log2(math.e)
         halves = [pl.ds(i * rows, rows) for i in (0, 1)]
 
@@ -235,30 +285,29 @@
             total = jnp.sum(total, axis=0, keepdims=True)
             lse[ch] = jnp.broadcast_to(top * factor + jnp.log2(total), (8, pair))
             inv = 1.0 / total
-            ot[...] = jnp.zeros_like(ot)
+            dqt[...] = jnp.zeros_like(dqt)
 
             def outputs(j, _):
-                ot[...] += dot(vt_all[j], (st[j] * inv).astype(BF16))
+                dqt[...] += dot(vo_all[j], (st[j] * inv).astype(BF16))
                 return 0
 
             lax.fori_loop(0, ch + 1, outputs, 0)
-            o_all[ch] = ot[...].astype(BF16)
+            vo_all[ch] = dqt[...].astype(BF16)
 
         def forwarded(u, _):
             @pl.when(u == hops)
             def _():
-                service(RW, 1)
-
-            forward(chip_at(u))
+                service(RY, 0)
+
+            forward(chips - 1 - u)
             return 0
 
-        service(RW, 0)
         lax.fori_loop(0, chips, forwarded, 0)
 
         def attend(ch):
             dot_s[...] = dot(dy_all[ch], wot[...]).astype(BF16).T
             qt_s[...] = q_all[ch].T
-            row = jnp.sum(dot_s[...].astype(F32) * o_all[ch].astype(F32), axis=0, keepdims=True)
+            row = jnp.sum(dot_s[...].astype(F32) * vo_all[ch].astype(F32), axis=0, keepdims=True)
             shift = lse[ch, 0:1, :]
             dqt[...] = jnp.zeros_like(dqt)
 
@@ -284,12 +333,14 @@
 
             lax.fori_loop(0, ch, grads, 0)
             tile(ch, True)
+            q_all[ch] = dqt[...].astype(BF16).T
+
+        def weight_grads(ch):
             dq = dqt[...].astype(BF16)
-            q_all[ch] = dq.T
             for t in range(width // pair):
                 at = pl.ds(t * pair, pair)
                 dwqt[:, at] += dot(dq, x_all[ch, :, at])
-                dwo_acc[:, at] += dot(o_all[ch], dy_all[ch, :, at])
+                dwo_acc[:, at] += dot(vo_all[ch], dy_all[ch, :, at])
 
         def send_dq(u, i):
             ch = chip_at(u)
@@ -299,23 +350,10 @@
             def _():
                 remote(q_all.at[ch, halves[i], :], dq_in.at[m], dq_s.at[blk], dq_r.at[m], blk).start()
 
-        late = chips - 1
-
         def attended(u, _):
-            @pl.when(u == 1)
-            def _():
-                for a in range(2, last - 1 - 2):
-                    service(RW, a)
-                service(RY, 0)
-
             @pl.when((u >= 1) & (u < last))
             def _():
                 service(RY, u)
-
-            @pl.when(u == last - 2)
-            def _():
-                service(RW, last - 2 - 1)
-                service(RW, last - 2 - 0)
 
             @pl.when(u == chips - 1)
             def _():
@@ -324,10 +362,12 @@
             wait_pair(RY, u)
             attend(chip_at(u))
 
-            @pl.when(u < late)
-            def _():
-                send_dq(u, 0)
-                send_dq(u, 1)
+            send_dq(u, 0)
+            send_dq(u, 1)
+
+            @pl.when(u < chips - 1)
+            def _():
+                weight_grads(chip_at(u))
 
             return 0
 
@@ -351,18 +391,7 @@
 
         for i in range(chips):
             px(i).start()
-        dwo_out = local(dwo_acc, dwo_hbm, 0)
-        dwo_out.start()
         spare = width // pair
-        dwq_out = []
-        for t in range(spare):
-            at = pl.ds(t * pair, pair)
-            staged = st.at[spare + t, :, pl.ds(0, dim)]
-            staged[...] = dwqt[:, at].T
-            out = local(staged, dwq_hbm.at[at, :], 6 + t)
-            out.start()
-            dwq_out.append(out)
-            st[t, pl.ds(0, rows), :] = jnp.zeros((rows, pair), F32)
 
         def add_dx(dq, w_ref):
             for t in range(spare):
@@ -383,10 +412,6 @@
 
         def dx_heads(lo, hi):
             def body(v, _):
-                @pl.when(lax.rem(v, 2) == 1)
-                def _():
-                    wait_pair(RW, lax.div(v, 2))
-
                 fetch(v).start()
 
                 @pl.when(v > 1)
@@ -426,17 +451,65 @@
 
         gather(0)
         hop(1)
-        service(RW, last - 1)
-        add_dx(q_all[c, own_rows, :], wqkv.at[:, pl.ds(0, dim)])
-        dx_heads(1, late + 3)
-        service(RW, last)
+        weight_grads(chip_at(chips - 1))
         for i in range(1, chips):
             gather(i)
         hop(2)
-        for t in range(3, hops):
+        dwo_out = local(dwo_acc, dwo_hbm, 0)
+        dwo_out.start()
+        dwq_out = []
+        for t in range(spare):
+            at = pl.ds(t * pair, pair)
+            staged = st.at[spare + t, :, pl.ds(0, dim)]
+            staged[...] = dwqt[:, at].T
+            out = local(staged, dwq_hbm.at[at, :], 6 + t)
+            out.start()
+            dwq_out.append(out)
+            st[t, pl.ds(0, rows), :] = jnp.zeros((rows, pair), F32)
+
+        add_dx(q_all[c, own_rows, :], wqkv.at[:, pl.ds(0, dim)])
+        gathered_weights()
+        dx_heads(1, 4)
+        done = 4
+        for t in range(3, hops + 1):
             hop(t)
-        dx_heads(late + 3, n - 2)
-        hop(hops)
+            dx_heads(done, done + 4)
+            done += 4
+
+        def tokens_of(dev):
+            chip = lax.div(dev, 2)
+            at = pl.ds(pl.multiple_of(lax.rem(dev, 2) * rows, rows), rows)
+            return thin.at[lax.div(chip, quarter), lax.rem(chip, quarter), :, at]
+
+        def kv_copy(dev):
+            return remote(tokens_of(dev), kv_rows.at[m], kv_s.at[dev], kv_r.at[m], dev)
+
+        def dw_copy(dev):
+            return remote(dw_out.at[dev], dw_in.at[m], dw_s.at[dev], dw_r.at[m], dev)
+
+        per = pair // cols
+
+        def key_grads(h):
+            def body(t, _):
+                at = pl.ds(pl.multiple_of(t * pair, pair), pair)
+                add = dot(thin[h, 0], x_all[h * quarter, :, at])
+                for j in range(1, quarter):
+                    add += dot(thin[h, j], x_all[h * quarter + j, :, at])
+                for i in range(per):
+                    dev = t * per + i
+                    piece = add[:, i * cols : (i + 1) * cols]
+                    dw_out[dev] = piece if h == 0 else dw_out[dev] + piece
+                if h == 1:
+                    for i in range(per):
+                        dev = t * per + i
+
+                        @pl.when(dev != m)
+                        def _():
+                            dw_copy(dev).start()
+
+                return 0
+
+            lax.fori_loop(0, width // pair, body, 0)
 
         for h in (0, 1):
             total = part[c, h]
@@ -446,48 +519,28 @@
                 total += held[...]
             thin[h] = total.astype(BF16)
 
-        def tokens_of(dev):
-            chip = lax.div(dev, 2)
-            at = pl.ds(pl.multiple_of(lax.rem(dev, 2) * rows, rows), rows)
-            return thin.at[lax.div(chip, quarter), lax.rem(chip, quarter), :, at]
-
-        def kv_copy(i):
-            dev = lax.rem(m + i, n)
-            return remote(tokens_of(dev), kv_rows.at[m], kv_s.at[i], kv_r.at[i], dev)
-
-        far = sorted(range(1, n), key=lambda i: -min(i, n - i))
-        for i in far:
-            kv_copy(i).start()
-        send_dq(chips - 1, 0)
-        send_dq(chips - 1, 1)
-        kv_rows[m] = tokens_of(m)[...]
-
-        def dw_copy(dev):
-            return remote(dw_out.at[dev], dw_in.at[m], dw_s.at[dev], dw_r.at[m], dev)
-
-        per = pair // cols
-
-        def key_grads(t, _):
-            at = pl.ds(pl.multiple_of(t * pair, pair), pair)
-            add = dot(thin[0, 0], x_all[0, :, at])
-            for j in range(1, chips):
-                add += dot(thin[j // quarter, j % quarter], x_all[j, :, at])
-            for i in range(per):
-                dw_out[t * per + i] = add[:, i * cols : (i + 1) * cols]
-            for i in range(per):
-                dev = t * per + i
-
+            def send_rows(dev, _):
                 @pl.when(dev != m)
                 def _():
-                    dw_copy(dev).start()
+                    kv_copy(dev).start()
+
+                return 0
+
+            lax.fori_loop(h * n // 2, (h + 1) * n // 2, send_rows, 0)
+            key_grads(h)
+        kv_rows[m] = tokens_of(m)[...]
+        dx_heads(done, n)
+        dx_head(n - 1)
+
+        def rows_arrived(dev, _):
+            @pl.when(dev != m)
+            def _():
+                kv_copy(dev).wait_send()
+                remote(kv_rows.at[dev], kv_rows.at[dev], kv_s.at[dev], kv_r.at[dev], mate).wait_recv()
 
             return 0
 
-        lax.fori_loop(0, width // pair, key_grads, 0)
-        dx_heads(n - 2, n)
-        dx_head(n - 1)
-        for i in far:
-            kv_copy(i).wait_recv()
+        lax.fori_loop(0, n, rows_arrived, 0)
         own_kv = kv_rows[...].reshape(2 * dim, rows).T
         wait_sends(RY)
         for t in range(spare):
@@ -518,8 +571,8 @@
 
         for r in (RX, RW):
             wait_sends(r)
-        for i in far:
-            kv_copy(i).wait_send()
+        for i in range(1, groups):
+            peer(i).wait_send()
         for i in range(chips):
             px(i).wait_send()
         for copy in sent:
@@ -561,6 +614,7 @@
 
 def solution(mesh):
     n = mesh.shape["model"]
+    groups = mesh.shape["data"]
     chips = n // 2
     hops = chips // 2
     tok_spec = P(("data", "model"), None)
@@ -575,7 +629,7 @@
         arrivals = 2 * hops - 1
         slim = 2 * dim // n
         outs = pl.pallas_call(
-            make_kernel(n),
+            make_kernel(n, groups),
             name="mqa_backward",
             out_shape=(
                 sds((rows, width), BF16),
@@ -594,10 +648,8 @@
                 vmem((2, chips, 2 * rows, dim), BF16),
                 vmem((chips, dim, 2 * rows), BF16),
                 vmem((chips, dim, 2 * rows), BF16),
-                vmem((chips, dim, 2 * rows), BF16),
                 vmem((chips, 8, 2 * rows), F32),
                 vmem((width, 3 * dim), BF16),
-                vmem((dim, width), BF16),
                 vmem((width, dim), BF16),
                 vmem((2, 2, hops, dim, 2 * rows), F32),
                 vmem((chips, 2, hops, slim, 2 * rows), F32),
@@ -607,7 +659,6 @@
                 vmem((dim, width), F32),
                 vmem((chips, 2 * rows, 2 * rows), F32),
                 vmem((2, width, dim), BF16),
-                vmem((dim, 2 * rows), F32),
                 vmem((dim, 2 * rows), F32),
                 vmem((dim, 2 * rows), BF16),
                 vmem((dim, 2 * rows), BF16),
@@ -630,6 +681,8 @@
                 dma((n,)),
                 dma((n,)),
                 dma((n,)),
+                dma((groups,)),
+                dma((groups,)),
                 dma((6 + width // (2 * rows),)),
             ],
             compiler_params=pltpu.CompilerParams(

time: 267 us -> 248 us (0.929)
  Pallas kernels: 265 us -> 247 us
    pallas_call x1, Pallas kernels: 261 us -> 243 us  [local_step(): pl.pallas_call(make_kernel(n, groups), name='mqa_backward', out_shape=(sd...]
where the time goes in v6:
time: 248 us
  Pallas kernels  247 us (100%)
    pallas_call x1, Pallas kernels, local_step(): pl.pallas_call(make_kernel(n, groups), name='mqa_backward', out_shape=(sd...  243 us

profile of v6, /device:TPU:21, one launch (start us, length us, event | category | flops | bytes accessed | tf_op | source)
XLA Modules:
  0.0 247.8 jit_solution(11433237148147153826)
XLA Ops:
  0.6 243.0 %mqa_backward.1 = (bf16[256,2048]{1,0:T(8,128)(2,1)}, f32[2048,128]{1,0:T(8,128)}, f32[128,128]{1,0:T(8,128)}, f32[128,128]{1,0:T(8,128)}, f32[128,2048]{1,0:T(8,128)}, /*index=5*/bf16[16,2048,128]{2,1,0:T(8,128)(2,1)}) custom-call(bf16[256,2048]{1,0:T(8,128)(2,1)} %x_hbm.1, bf16[256,2048]{1,0:T(8,128)(2,1)} %dy_hbm.1, bf16[2048,128]{1,0:T(8,128)(2,1)} %bitcast.6, ...), custom_call_target="tpu_custom_call" | custom-call | tf_op jit(solution)/shard_map/mqa_backward/pallas_call | solution.py:631
  243.6 4.2 %hand_on.1 = (bf16[256,2048]{1,0:T(8,128)(2,1)}, f32[2048,128]{1,0:T(8,128)}, f32[128,128]{1,0:T(8,128)}, f32[128,128]{1,0:T(8,128)}, f32[128,2048]{1,0:T(8,128)}) custom-call(bf16[256,2048]{1,0:T(8,128)(2,1)} %get-tuple-element.15.refs_0_, f32[2048,128]{1,0:T(8,128)} %get-tuple-element.16.refs_1_, f32[128,128]{1,0:T(8,128)} %get-tuple-element.17.refs_2_, ...), custom_call_target="tpu_custom_call" | custom-call | tf_op jit(solution)/shard_map/hand_on/pallas_call | solution.py:701

commit v7 on v6

--- a/solution.py
+++ b/solution.py
@@ -230,6 +230,7 @@
             @pl.when(u == hops)
             def _():
                 service(RW, last)
+                spread()
 
             @pl.when((u >= 1) & (u <= last))
             def _():
@@ -238,10 +239,6 @@
             @pl.when(u == last - 2)
             def _():
                 start_own(RY)
-
-            @pl.when(u == hops + 1)
-            def _():
-                spread()
 
             wait_pair(RX, u)
             project(chip_at(u))
@@ -295,9 +292,13 @@
             vo_all[ch] = dqt[...].astype(BF16)
 
         def forwarded(u, _):
-            @pl.when(u == hops)
+            @pl.when(u == 2)
             def _():
                 service(RY, 0)
+
+            @pl.when(u == chips - 2)
+            def _():
+                service(RY, 1)
 
             forward(chips - 1 - u)
             return 0
@@ -350,8 +351,50 @@
             def _():
                 remote(q_all.at[ch, halves[i], :], dq_in.at[m], dq_s.at[blk], dq_r.at[m], blk).start()
 
+            @pl.when(blk == m)
+            def _():
+                dq_in[m] = q_all[ch, halves[i], :]
+
+        spare = width // pair
+
+        def fetch(u, i):
+            slot = lax.rem(u, 2)
+            dst = wq_st.at[slot, :, pl.ds(i * dim, dim)]
+            return local(wq_all.at[2 * chip_at(u) + i], dst, 2 + 2 * slot + i)
+
+        def dx_start(u):
+            fetch(u, 0).start()
+            fetch(u, 1).start()
+
+        def dx_pair(u):
+            dq = []
+            for i in (0, 1):
+                h = 2 * chip_at(u) + i
+                fetch(u, i).wait()
+
+                @pl.when(h != m)
+                def _():
+                    remote(dq_in.at[h], dq_in.at[h], dq_s.at[h], dq_r.at[h], mate).wait_recv()
+
+                dq.append(dq_in[h])
+            dq = jnp.concatenate(dq, axis=1)
+            for t in range(spare):
+                at = pl.ds(t * pair, pair)
+                st[t, pl.ds(0, rows), :] += dot_nt(dq, wq_st[lax.rem(u, 2), at, :])
+
+        def dx_pairs(lo, hi):
+            def body(u, _):
+                @pl.when(u + 1 < chips)
+                def _():
+                    dx_start(u + 1)
+
+                dx_pair(u)
+                return 0
+
+            lax.fori_loop(lo, hi, body, 0)
+
         def attended(u, _):
-            @pl.when((u >= 1) & (u < last))
+            @pl.when((u >= 2) & (u < last))
             def _():
                 service(RY, u)
 
@@ -362,8 +405,15 @@
             wait_pair(RY, u)
             attend(chip_at(u))
 
-            send_dq(u, 0)
-            send_dq(u, 1)
+            @pl.when(u == chips - 2)
+            def _():
+                send_dq(chips - 3, 0)
+                send_dq(chips - 3, 1)
+
+            @pl.when(u != chips - 3)
+            def _():
+                send_dq(u, 0)
+                send_dq(u, 1)
 
             @pl.when(u < chips - 1)
             def _():
@@ -391,36 +441,6 @@
 
         for i in range(chips):
             px(i).start()
-        spare = width // pair
-
-        def add_dx(dq, w_ref):
-            for t in range(spare):
-                st[t, pl.ds(0, rows), :] += dot_nt(dq, w_ref[pl.ds(t * pair, pair), :])
-
-        def head_at(v):
-            return 2 * chip_at(lax.div(v, 2)) + lax.rem(k + lax.rem(v, 2), 2)
-
-        def fetch(v):
-            slot = lax.rem(v, 2)
-            return local(wq_all.at[head_at(v)], wq_st.at[slot], 2 + slot)
-
-        def dx_head(v):
-            h = head_at(v)
-            fetch(v).wait()
-            remote(dq_in.at[h], dq_in.at[h], dq_s.at[h], dq_r.at[h], mate).wait_recv()
-            add_dx(dq_in[h], wq_st.at[lax.rem(v, 2)])
-
-        def dx_heads(lo, hi):
-            def body(v, _):
-                fetch(v).start()
-
-                @pl.when(v > 1)
-                def _():
-                    dx_head(v - 1)
-
-                return 0
-
-            lax.fori_loop(lo, hi, body, 0)
 
         def gather(i):
             px(i).wait_recv()
@@ -452,6 +472,11 @@
         gather(0)
         hop(1)
         weight_grads(chip_at(chips - 1))
+        gathered_weights()
+        for t in range(spare):
+            st[t, pl.ds(0, rows), :] = jnp.zeros((rows, pair), F32)
+        dx_start(0)
+        dx_pairs(0, 5)
         for i in range(1, chips):
             gather(i)
         hop(2)
@@ -465,16 +490,12 @@
             out = local(staged, dwq_hbm.at[at, :], 6 + t)
             out.start()
             dwq_out.append(out)
-            st[t, pl.ds(0, rows), :] = jnp.zeros((rows, pair), F32)
-
-        add_dx(q_all[c, own_rows, :], wqkv.at[:, pl.ds(0, dim)])
-        gathered_weights()
-        dx_heads(1, 4)
-        done = 4
-        for t in range(3, hops + 1):
-            hop(t)
-            dx_heads(done, done + 4)
-            done += 4
+
+        dx_pairs(5, 6)
+        hop(hops - 1)
+        dx_pairs(6, 7)
+        hop(hops)
+        dx_pairs(7, 7)
 
         def tokens_of(dev):
             chip = lax.div(dev, 2)
@@ -529,8 +550,7 @@
             lax.fori_loop(h * n // 2, (h + 1) * n // 2, send_rows, 0)
             key_grads(h)
         kv_rows[m] = tokens_of(m)[...]
-        dx_heads(done, n)
-        dx_head(n - 1)
+        dx_pairs(7, chips)
 
         def rows_arrived(dev, _):
             @pl.when(dev != m)
@@ -658,7 +678,7 @@
                 vmem((dim, width), F32),
                 vmem((dim, width), F32),
                 vmem((chips, 2 * rows, 2 * rows), F32),
-                vmem((2, width, dim), BF16),
+                vmem((2, width, 2 * dim), BF16),
                 vmem((dim, 2 * rows), F32),
                 vmem((dim, 2 * rows), BF16),
                 vmem((dim, 2 * rows), BF16),

time: 248 us -> 244 us (0.984)
  Pallas kernels: 247 us -> 243 us
    pallas_call x1, Pallas kernels: 243 us -> 239 us  [local_step(): pl.pallas_call(make_kernel(n, groups), name='mqa_backward', out_shape=(sd...]
where the time goes in v7:
time: 244 us; the launch traced here: 243 us
  Pallas kernels  243 us (100%)
    pallas_call x1, Pallas kernels, local_step(): pl.pallas_call(make_kernel(n, groups), name='mqa_backward', out_shape=(sd...  239 us

profile of v7, /device:TPU:21, one launch (start us, length us, event | category | flops | bytes accessed | tf_op | source)
XLA Modules:
  0.0 243.4 jit_solution(16459989583950142058)
XLA Ops:
  0.6 238.5 %mqa_backward.1 = (bf16[256,2048]{1,0:T(8,128)(2,1)}, f32[2048,128]{1,0:T(8,128)}, f32[128,128]{1,0:T(8,128)}, f32[128,128]{1,0:T(8,128)}, f32[128,2048]{1,0:T(8,128)}, /*index=5*/bf16[16,2048,128]{2,1,0:T(8,128)(2,1)}) custom-call(bf16[256,2048]{1,0:T(8,128)(2,1)} %x_hbm.1, bf16[256,2048]{1,0:T(8,128)(2,1)} %dy_hbm.1, bf16[2048,128]{1,0:T(8,128)(2,1)} %bitcast.6, ...), custom_call_target="tpu_custom_call" | custom-call | tf_op jit(solution)/shard_map/mqa_backward/pallas_call | solution.py:651
  239.1 4.2 %hand_on.1 = (bf16[256,2048]{1,0:T(8,128)(2,1)}, f32[2048,128]{1,0:T(8,128)}, f32[128,128]{1,0:T(8,128)}, f32[128,128]{1,0:T(8,128)}, f32[128,2048]{1,0:T(8,128)}) custom-call(bf16[256,2048]{1,0:T(8,128)(2,1)} %get-tuple-element.15.refs_0_, f32[2048,128]{1,0:T(8,128)} %get-tuple-element.16.refs_1_, f32[128,128]{1,0:T(8,128)} %get-tuple-element.17.refs_2_, ...), custom_call_target="tpu_custom_call" | custom-call | tf_op jit(solution)/shard_map/hand_on/pallas_call | solution.py:721

commit v8 on v7

--- a/solution.py
+++ b/solution.py
@@ -315,15 +315,21 @@
             def tile(j, masked):
                 add_q = 0.0
                 hi, lo = lax.div(j, quarter), lax.rem(j, quarter)
+                step = rows // 2
                 for i in (0, 1):
+                    ps, gs = [], []
+                    for b in (0, 1):
+                        at = pl.ds(i * rows + b * step, step)
+                        s = dot(kv_all[0, j, at, :], qt_s[...])
+                        dp = dot(kv_all[1, j, at, :], dot_s[...])
+                        p = jnp.exp2(s * factor - shift)
+                        if masked:
+                            p = jnp.where(causal(i)[b * step : (b + 1) * step], p, 0.0)
+                        ps.append(p.astype(BF16))
+                        gs.append((p * (dp - row) * scale).astype(BF16))
                     at = halves[i]
-                    s = dot(kv_all[0, j, at, :], qt_s[...])
-                    p = jnp.exp2(s * factor - shift)
-                    if masked:
-                        p = jnp.where(causal(i), p, 0.0)
-                    dp = dot(kv_all[1, j, at, :], dot_s[...])
-                    g = (p * (dp - row) * scale).astype(BF16)
-                    dkv[1, hi, lo, :, at] += dot_nt(dot_s[...], p.astype(BF16))
+                    g = jnp.concatenate(gs, axis=0)
+                    dkv[1, hi, lo, :, at] += dot_nt(dot_s[...], jnp.concatenate(ps, axis=0))
                     dkv[0, hi, lo, :, at] += dot_nt(qt_s[...], g)
                     add_q += dot(kt_all[j, :, at], g)
                 dqt[...] += add_q
@@ -447,25 +453,29 @@
             chip = chip_off(order[i])
             part[chip] += slice_of(2 * chip + k)[...]
 
-        def rs(d, t, h, src):
-            return remote(src, sums.at[d, t - 1, h], rs_s.at[d, t - 1, h], rs_r.at[d, t - 1, h], nbr[d])
+        few = quarter // 2
+
+        def piece(ref, q):
+            return ref.at[q // 2, pl.ds(q % 2 * few, few)]
+
+        def rs(d, t, q, src):
+            return remote(src, piece(sums.at[d, t - 1], q), rs_s.at[d, t - 1, q], rs_r.at[d, t - 1, q], nbr[d])
 
         sent = []
 
         def hop(t):
-            for first in (True, False):
+            for q in range(4):
                 for d in (0, 1):
-                    h = d if first else 1 - d
                     chip = chip_off((hops + 1 - t) * (1 - 2 * d))
-                    if t == 1 and not first:
+                    if t == 1 and q // 2 != d:
                         continue
-                    if t == 1 or (t == 2 and not first):
-                        copy = rs(d, t, h, part.at[chip, h])
+                    if t == 1 or (t == 2 and q // 2 != d):
+                        copy = rs(d, t, q, piece(part.at[chip], q))
                     else:
-                        held = sums.at[d, t - 2, h]
-                        rs(d, t - 1, h, held).wait_recv()
-                        held[...] += part[chip, h]
-                        copy = rs(d, t, h, held)
+                        held = piece(sums.at[d, t - 2], q)
+                        rs(d, t - 1, q, held).wait_recv()
+                        held[...] += piece(part.at[chip], q)[...]
+                        copy = rs(d, t, q, held)
                     copy.start()
                     sent.append(copy)
 
@@ -535,9 +545,9 @@
         for h in (0, 1):
             total = part[c, h]
             for d in (0, 1):
-                held = sums.at[d, hops - 1, h]
-                rs(d, hops, h, held).wait_recv()
-                total += held[...]
+                for q in (2 * h, 2 * h + 1):
+                    rs(d, hops, q, piece(sums.at[d, hops - 1], q)).wait_recv()
+                total += sums[d, hops - 1, h]
             thin[h] = total.astype(BF16)
 
             def send_rows(dev, _):
@@ -616,7 +626,7 @@
     sems_in, sems_out = refs[3 * count :]
     pieces = []
     for src, dst, buf in zip(srcs, dsts, bufs):
-        parts = max(1, src.shape[0] * src.shape[1] // (1 << 16))
+        parts = max(1, src.shape[0] * src.shape[1] // (1 << 17))
         size = src.shape[0] // parts
         for i in range(parts):
             at = pl.ds(i * size, size)
@@ -695,8 +705,8 @@
                 dma((n,)),
                 dma((chips,)),
                 dma((chips,)),
-                dma((2, hops, 2)),
-                dma((2, hops, 2)),
+                dma((2, hops, 4)),
+                dma((2, hops, 4)),
                 dma((n,)),
                 dma((n,)),
                 dma((n,)),

time: 244 us -> 241 us (0.988)
  Pallas kernels: 243 us -> 240 us
    pallas_call x1, Pallas kernels: 239 us -> 236 us  [local_step(): pl.pallas_call(make_kernel(n, groups), name='mqa_backward', out_shape=(sd...]
where the time goes in v8:
time: 241 us; the launch traced here: 240 us
  Pallas kernels  240 us (100%)
    pallas_call x1, Pallas kernels, local_step(): pl.pallas_call(make_kernel(n, groups), name='mqa_backward', out_shape=(sd...  236 us

profile of v8, /device:TPU:21, one launch (start us, length us, event | category | flops | bytes accessed | tf_op | source)
XLA Modules:
  0.0 240.5 jit_solution(4257259957984068767)
XLA Ops:
  0.6 236.0 %mqa_backward.1 = (bf16[256,2048]{1,0:T(8,128)(2,1)}, f32[2048,128]{1,0:T(8,128)}, f32[128,128]{1,0:T(8,128)}, f32[128,128]{1,0:T(8,128)}, f32[128,2048]{1,0:T(8,128)}, /*index=5*/bf16[16,2048,128]{2,1,0:T(8,128)(2,1)}) custom-call(bf16[256,2048]{1,0:T(8,128)(2,1)} %x_hbm.1, bf16[256,2048]{1,0:T(8,128)(2,1)} %dy_hbm.1, bf16[2048,128]{1,0:T(8,128)(2,1)} %bitcast.6, ...), custom_call_target="tpu_custom_call" | custom-call | tf_op jit(solution)/shard_map/mqa_backward/pallas_call | solution.py:661
  236.6 3.9 %hand_on.1 = (bf16[256,2048]{1,0:T(8,128)(2,1)}, f32[2048,128]{1,0:T(8,128)}, f32[128,128]{1,0:T(8,128)}, f32[128,128]{1,0:T(8,128)}, f32[128,2048]{1,0:T(8,128)}) custom-call(bf16[256,2048]{1,0:T(8,128)(2,1)} %get-tuple-element.15.refs_0_, f32[2048,128]{1,0:T(8,128)} %get-tuple-element.16.refs_1_, f32[128,128]{1,0:T(8,128)} %get-tuple-element.17.refs_2_, ...), custom_call_target="tpu_custom_call" | custom-call | tf_op jit(solution)/shard_map/hand_on/pallas_call | solution.py:731

commit v9 on v8

--- a/solution.py
+++ b/solution.py
@@ -39,7 +39,7 @@
     def kernel(
         x_hbm, dy_hbm, wq_hbm, wk_hbm, wv_hbm, wo_hbm,
         dx_hbm, dwq_hbm, dwk_hbm, dwv_hbm, dwo_hbm, wq_all,
-        x_all, dy_all, q_all, kv_all, kt_all, vo_all, lse, wqkv, wot,
+        x_all, dy_all, q_all, kv_all, kt_all, vo_all, soft, wqkv, wot,
         dkv, part, sums, dq_in, dwqt, dwo_acc, st, wq_st,
         dqt, dot_s, qt_s, thin, kv_rows, dw_out, dw_in, dw_t,
         ring_r, ring_s, pair_r, pair_s, dq_r, dq_s, px_r, px_s, rs_r, rs_s,
@@ -280,8 +280,9 @@
 
             total = lax.fori_loop(0, ch + 1, weights, jnp.zeros((8, pair), F32))
             total = jnp.sum(total, axis=0, keepdims=True)
-            lse[ch] = jnp.broadcast_to(top * factor + jnp.log2(total), (8, pair))
             inv = 1.0 / total
+            soft[ch, 0] = jnp.broadcast_to(top, (8, pair))
+            soft[ch, 1] = jnp.broadcast_to(inv, (8, pair))
             dqt[...] = jnp.zeros_like(dqt)
 
             def outputs(j, _):
@@ -309,7 +310,7 @@
             dot_s[...] = dot(dy_all[ch], wot[...]).astype(BF16).T
             qt_s[...] = q_all[ch].T
             row = jnp.sum(dot_s[...].astype(F32) * vo_all[ch].astype(F32), axis=0, keepdims=True)
-            shift = lse[ch, 0:1, :]
+            top, inv = soft[ch, 0, 0:1, :], soft[ch, 1, 0:1, :]
             dqt[...] = jnp.zeros_like(dqt)
 
             def tile(j, masked):
@@ -322,7 +323,7 @@
                         at = pl.ds(i * rows + b * step, step)
                         s = dot(kv_all[0, j, at, :], qt_s[...])
                         dp = dot(kv_all[1, j, at, :], dot_s[...])
-                        p = jnp.exp2(s * factor - shift)
+                        p = jnp.exp2((s - top) * factor) * inv
                         if masked:
                             p = jnp.where(causal(i)[b * step : (b + 1) * step], p, 0.0)
                         ps.append(p.astype(BF16))
@@ -407,14 +408,11 @@
             @pl.when(u == chips - 1)
             def _():
                 service(RY, last)
+                send_dq(chips - 3, 0)
+                send_dq(chips - 3, 1)
 
             wait_pair(RY, u)
             attend(chip_at(u))
-
-            @pl.when(u == chips - 2)
-            def _():
-                send_dq(chips - 3, 0)
-                send_dq(chips - 3, 1)
 
             @pl.when(u != chips - 3)
             def _():
@@ -678,7 +676,7 @@
                 vmem((2, chips, 2 * rows, dim), BF16),
                 vmem((chips, dim, 2 * rows), BF16),
                 vmem((chips, dim, 2 * rows), BF16),
-                vmem((chips, 8, 2 * rows), F32),
+                vmem((chips, 2, 8, 2 * rows), F32),
                 vmem((width, 3 * dim), BF16),
                 vmem((width, dim), BF16),
                 vmem((2, 2, hops, dim, 2 * rows), F32),

time: 241 us -> 242 us (level)
  no operation moved by 1% of the time
where the time goes in v9:
time: 242 us; the launch traced here: 241 us
  Pallas kernels  241 us (100%)
    pallas_call x1, Pallas kernels, local_step(): pl.pallas_call(make_kernel(n, groups), name='mqa_backward', out_shape=(sd...  237 us

profile of v9, /device:TPU:21, one launch (start us, length us, event | category | flops | bytes accessed | tf_op | source)
XLA Modules:
  0.0 241.3 jit_solution(1950824559059976838)
XLA Ops:
  0.6 236.8 %mqa_backward.1 = (bf16[256,2048]{1,0:T(8,128)(2,1)}, f32[2048,128]{1,0:T(8,128)}, f32[128,128]{1,0:T(8,128)}, f32[128,128]{1,0:T(8,128)}, f32[128,2048]{1,0:T(8,128)}, /*index=5*/bf16[16,2048,128]{2,1,0:T(8,128)(2,1)}) custom-call(bf16[256,2048]{1,0:T(8,128)(2,1)} %x_hbm.1, bf16[256,2048]{1,0:T(8,128)(2,1)} %dy_hbm.1, bf16[2048,128]{1,0:T(8,128)(2,1)} %bitcast.6, ...), custom_call_target="tpu_custom_call" | custom-call | tf_op jit(solution)/shard_map/mqa_backward/pallas_call | solution.py:659
  237.5 3.9 %hand_on.1 = (bf16[256,2048]{1,0:T(8,128)(2,1)}, f32[2048,128]{1,0:T(8,128)}, f32[128,128]{1,0:T(8,128)}, f32[128,128]{1,0:T(8,128)}, f32[128,2048]{1,0:T(8,128)}) custom-call(bf16[256,2048]{1,0:T(8,128)(2,1)} %get-tuple-element.15.refs_0_, f32[2048,128]{1,0:T(8,128)} %get-tuple-element.16.refs_1_, f32[128,128]{1,0:T(8,128)} %get-tuple-element.17.refs_2_, ...), custom_call_target="tpu_custom_call" | custom-call | tf_op jit(solution)/shard_map/hand_on/pallas_call | solution.py:729

commit v10 on v9

--- a/solution.py
+++ b/solution.py
@@ -314,26 +314,32 @@
             dqt[...] = jnp.zeros_like(dqt)
 
             def tile(j, masked):
-                add_q = 0.0
+                add_q = []
                 hi, lo = lax.div(j, quarter), lax.rem(j, quarter)
                 step = rows // 2
                 for i in (0, 1):
+                    first = i * rows if masked else 0
+                    ask = pl.ds(first, pair - first)
                     ps, gs = [], []
                     for b in (0, 1):
                         at = pl.ds(i * rows + b * step, step)
-                        s = dot(kv_all[0, j, at, :], qt_s[...])
-                        dp = dot(kv_all[1, j, at, :], dot_s[...])
-                        p = jnp.exp2((s - top) * factor) * inv
+                        s = dot(kv_all[0, j, at, :], qt_s[:, ask])
+                        dp = dot(kv_all[1, j, at, :], dot_s[:, ask])
+                        p = jnp.exp2((s - top[:, first:]) * factor) * inv[:, first:]
                         if masked:
-                            p = jnp.where(causal(i)[b * step : (b + 1) * step], p, 0.0)
+                            p = jnp.where(causal(0)[b * step : (b + 1) * step, : pair - first], p, 0.0)
                         ps.append(p.astype(BF16))
-                        gs.append((p * (dp - row) * scale).astype(BF16))
+                        gs.append((p * (dp - row[:, first:]) * scale).astype(BF16))
                     at = halves[i]
                     g = jnp.concatenate(gs, axis=0)
-                    dkv[1, hi, lo, :, at] += dot_nt(dot_s[...], jnp.concatenate(ps, axis=0))
-                    dkv[0, hi, lo, :, at] += dot_nt(qt_s[...], g)
-                    add_q += dot(kt_all[j, :, at], g)
-                dqt[...] += add_q
+                    dkv[1, hi, lo, :, at] += dot_nt(dot_s[:, ask], jnp.concatenate(ps, axis=0))
+                    dkv[0, hi, lo, :, at] += dot_nt(qt_s[:, ask], g)
+                    add_q.append(dot(kt_all[j, :, at], g))
+                if masked:
+                    dqt[...] += add_q[0]
+                    dqt[:, halves[1]] += add_q[1]
+                else:
+                    dqt[...] += add_q[0] + add_q[1]
 
             def grads(j, _):
                 tile(j, False)

time: 242 us -> 241 us (level)
  no operation moved by 1% of the time
where the time goes in v10:
time: 241 us
  Pallas kernels  240 us (100%)
    pallas_call x1, Pallas kernels, local_step(): pl.pallas_call(make_kernel(n, groups), name='mqa_backward', out_shape=(sd...  236 us

profile of v10, /device:TPU:21, one launch (start us, length us, event | category | flops | bytes accessed | tf_op | source)
XLA Modules:
  0.0 240.9 jit_solution(16609003415396670127)
XLA Ops:
  0.6 236.4 %mqa_backward.1 = (bf16[256,2048]{1,0:T(8,128)(2,1)}, f32[2048,128]{1,0:T(8,128)}, f32[128,128]{1,0:T(8,128)}, f32[128,128]{1,0:T(8,128)}, f32[128,2048]{1,0:T(8,128)}, /*index=5*/bf16[16,2048,128]{2,1,0:T(8,128)(2,1)}) custom-call(bf16[256,2048]{1,0:T(8,128)(2,1)} %x_hbm.1, bf16[256,2048]{1,0:T(8,128)(2,1)} %dy_hbm.1, bf16[2048,128]{1,0:T(8,128)(2,1)} %bitcast.6, ...), custom_call_target="tpu_custom_call" | custom-call | tf_op jit(solution)/shard_map/mqa_backward/pallas_call | solution.py:665
  237.0 3.9 %hand_on.1 = (bf16[256,2048]{1,0:T(8,128)(2,1)}, f32[2048,128]{1,0:T(8,128)}, f32[128,128]{1,0:T(8,128)}, f32[128,128]{1,0:T(8,128)}, f32[128,2048]{1,0:T(8,128)}) custom-call(bf16[256,2048]{1,0:T(8,128)(2,1)} %get-tuple-element.15.refs_0_, f32[2048,128]{1,0:T(8,128)} %get-tuple-element.16.refs_1_, f32[128,128]{1,0:T(8,128)} %get-tuple-element.17.refs_2_, ...), custom_call_target="tpu_custom_call" | custom-call | tf_op jit(solution)/shard_map/hand_on/pallas_call | solution.py:735

commit v11 on v10

--- a/solution.py
+++ b/solution.py
@@ -485,7 +485,6 @@
 
         gather(0)
         hop(1)
-        weight_grads(chip_at(chips - 1))
         gathered_weights()
         for t in range(spare):
             st[t, pl.ds(0, rows), :] = jnp.zeros((rows, pair), F32)
@@ -494,6 +493,7 @@
         for i in range(1, chips):
             gather(i)
         hop(2)
+        weight_grads(chip_at(chips - 1))
         dwo_out = local(dwo_acc, dwo_hbm, 0)
         dwo_out.start()
         dwq_out = []

time: 241 us -> 240 us (level)
  no operation moved by 1% of the time
where the time goes in v11:
time: 240 us
  Pallas kernels  239 us (100%)
    pallas_call x1, Pallas kernels, local_step(): pl.pallas_call(make_kernel(n, groups), name='mqa_backward', out_shape=(sd...  236 us

profile of v11, /device:TPU:21, one launch (start us, length us, event | category | flops | bytes accessed | tf_op | source)
XLA Modules:
  0.0 240.1 jit_solution(2263756938061602158)
XLA Ops:
  0.6 235.6 %mqa_backward.1 = (bf16[256,2048]{1,0:T(8,128)(2,1)}, f32[2048,128]{1,0:T(8,128)}, f32[128,128]{1,0:T(8,128)}, f32[128,128]{1,0:T(8,128)}, f32[128,2048]{1,0:T(8,128)}, /*index=5*/bf16[16,2048,128]{2,1,0:T(8,128)(2,1)}) custom-call(bf16[256,2048]{1,0:T(8,128)(2,1)} %x_hbm.1, bf16[256,2048]{1,0:T(8,128)(2,1)} %dy_hbm.1, bf16[2048,128]{1,0:T(8,128)(2,1)} %bitcast.6, ...), custom_call_target="tpu_custom_call" | custom-call | tf_op jit(solution)/shard_map/mqa_backward/pallas_call | solution.py:665
  236.2 3.9 %hand_on.1 = (bf16[256,2048]{1,0:T(8,128)(2,1)}, f32[2048,128]{1,0:T(8,128)}, f32[128,128]{1,0:T(8,128)}, f32[128,128]{1,0:T(8,128)}, f32[128,2048]{1,0:T(8,128)}) custom-call(bf16[256,2048]{1,0:T(8,128)(2,1)} %get-tuple-element.15.refs_0_, f32[2048,128]{1,0:T(8,128)} %get-tuple-element.16.refs_1_, f32[128,128]{1,0:T(8,128)} %get-tuple-element.17.refs_2_, ...), custom_call_target="tpu_custom_call" | custom-call | tf_op jit(solution)/shard_map/hand_on/pallas_call | solution.py:735

commit v12 on v11

--- a/solution.py
+++ b/solution.py
@@ -494,6 +494,10 @@
             gather(i)
         hop(2)
         weight_grads(chip_at(chips - 1))
+        dx_pairs(5, 6)
+        hop(hops - 1)
+        dx_pairs(6, 7)
+        hop(hops)
         dwo_out = local(dwo_acc, dwo_hbm, 0)
         dwo_out.start()
         dwq_out = []
@@ -505,10 +509,6 @@
             out.start()
             dwq_out.append(out)
 
-        dx_pairs(5, 6)
-        hop(hops - 1)
-        dx_pairs(6, 7)
-        hop(hops)
         dx_pairs(7, 7)
 
         def tokens_of(dev):

time: 240 us -> 240 us (level)
  no operation moved by 1% of the time
where the time goes in v12:
time: 240 us
  Pallas kernels  239 us (100%)
    pallas_call x1, Pallas kernels, local_step(): pl.pallas_call(make_kernel(n, groups), name='mqa_backward', out_shape=(sd...  236 us

profile of v12, /device:TPU:21, one launch (start us, length us, event | category | flops | bytes accessed | tf_op | source)
XLA Modules:
  0.0 240.1 jit_solution(18428663651782997190)
XLA Ops:
  0.6 235.6 %mqa_backward.1 = (bf16[256,2048]{1,0:T(8,128)(2,1)}, f32[2048,128]{1,0:T(8,128)}, f32[128,128]{1,0:T(8,128)}, f32[128,128]{1,0:T(8,128)}, f32[128,2048]{1,0:T(8,128)}, /*index=5*/bf16[16,2048,128]{2,1,0:T(8,128)(2,1)}) custom-call(bf16[256,2048]{1,0:T(8,128)(2,1)} %x_hbm.1, bf16[256,2048]{1,0:T(8,128)(2,1)} %dy_hbm.1, bf16[2048,128]{1,0:T(8,128)(2,1)} %bitcast.6, ...), custom_call_target="tpu_custom_call" | custom-call | tf_op jit(solution)/shard_map/mqa_backward/pallas_call | solution.py:665
  236.2 3.9 %hand_on.1 = (bf16[256,2048]{1,0:T(8,128)(2,1)}, f32[2048,128]{1,0:T(8,128)}, f32[128,128]{1,0:T(8,128)}, f32[128,128]{1,0:T(8,128)}, f32[128,2048]{1,0:T(8,128)}) custom-call(bf16[256,2048]{1,0:T(8,128)(2,1)} %get-tuple-element.15.refs_0_, f32[2048,128]{1,0:T(8,128)} %get-tuple-element.16.refs_1_, f32[128,128]{1,0:T(8,128)} %get-tuple-element.17.refs_2_, ...), custom_call_target="tpu_custom_call" | custom-call | tf_op jit(solution)/shard_map/hand_on/pallas_call | solution.py:735
